TPU v7x, 256 devices: a whole 4x4x8 slice. The times are simulated.
256 devices in a mesh: pair: 64 (over z, x, core), mp: 4 (over y).
Axes of the slice: x: 4, y: 4, z: 8, core: 2. Of those that a mesh axis runs over, the one named last changes fastest.
Arguments:
- current: bfloat16 [128, 196, 1024], P('pair'), may hold values from -6 to 6
- past_tokens: bfloat16 [128, 196, 1024], P('pair'), may hold values from -6 to 6
- counts: int32 [128], P('pair'), may hold values from 1 to 196, as said below
- partners: int32 [128], replicated, may hold values from 0 to 127, as said below
- query_weight: bfloat16 [1024, 1024], P(None, 'mp'), may hold values from -1.2 to 1.2
- key_weight: bfloat16 [1024, 1024], P(None, 'mp'), may hold values from -1.2 to 1.2
- value_weight: bfloat16 [1024, 1024], P(None, 'mp'), may hold values from -0.1875 to 0.1875
- output_weight: bfloat16 [1024, 1024], P('mp'), may hold values from -0.1875 to 0.1875
- up_weight: bfloat16 [1024, 4096], P(None, 'mp'), may hold values from -0.1875 to 0.1875
- down_weight: bfloat16 [4096, 1024], P('mp'), may hold values from -0.09375 to 0.09375
Outputs:
- decoded: bfloat16 [128, 196, 1024], P('pair', None, 'mp')
Inputs may be any that keep to these rules, and one draw needn't show every extreme that they name: counts[p] is at most 196; some pair has exactly 196. A permutation of the pairs; partners[p] % 2 == p % 2; the partners of the 2 pairs of one pair index lie on distinct pair indices, and the pairs whose partners lie on one pair index come from distinct pair indices.
All inputs are finite; a program needn't handle non-finite values.
Results may differ from a plain program's by a relative error of at most 0.0085.
Values may be sent and summed in bfloat16 or wider, within the bound.
A program may use at most 128 MiB of HBM per device.

v0:
```python
import jax
import jax.numpy as jnp
from jax import lax
from jax.sharding import PartitionSpec as P

HEAD_DIM = 64


def in_one_piece(arrays, axis, dim, along):
    widths = [a.shape[along] for a in arrays]
    both = jnp.concatenate(arrays, axis=along)
    result = lax.all_gather(both, axis, axis=dim, tiled=True)
    return tuple(jnp.split(result, [sum(widths[:k]) for k in range(1, len(widths))], axis=along))


def laid_out(blocks, dim):
    shape = list(blocks.shape[1:])
    shape[dim] *= blocks.shape[0]
    return jnp.moveaxis(blocks, 0, dim).reshape(shape)


def sent_to_all(array, axis):
    copies = jnp.broadcast_to(array, (lax.axis_size(axis), *array.shape))
    return lax.all_to_all(copies, axis, split_axis=0, concat_axis=0, tiled=True)


def gathered_copies(array, axis, dim):
    return laid_out(sent_to_all(array, axis), dim)


def split_up(array, dim, size):
    shape = array.shape
    blocks = array.reshape(*shape[:dim], size, shape[dim] // size, *shape[dim + 1 :])
    return jnp.moveaxis(blocks, dim, 0)


def summed_on_arrival(array, axis, dim):
    blocks = split_up(array, dim, lax.axis_size(axis))
    arrived = lax.all_to_all(blocks, axis, split_axis=0, concat_axis=0, tiled=True)
    return arrived.astype(jnp.float32).sum(axis=0)


def layer_norm(values):
    center = values - jnp.mean(values, axis=-1, keepdims=True)
    spread = jnp.mean(center * center, axis=-1, keepdims=True)
    return center * lax.rsqrt(spread + 1e-06)


def body(
    current,
    past_tokens,
    counts,
    partners,
    query_weight,
    key_weight,
    value_weight,
    output_weight,
    up_weight,
    down_weight,
):
    pair_count, slot_count, model_width = current.shape
    key_count = past_tokens.shape[1]
    features = query_weight.shape[1]
    head_local = features // HEAD_DIM
    row_count = pair_count * slot_count
    shards = lax.axis_size("mp")
    share_width = model_width // shards
    column_start = lax.axis_index("mp") * share_width
    normed = layer_norm(current.astype(jnp.float32).reshape(row_count, model_width)).astype(
        jnp.bfloat16
    )
    context = layer_norm(
        past_tokens.astype(jnp.float32).reshape(pair_count * key_count, model_width)
    ).astype(jnp.bfloat16)
    queries = jnp.dot(normed, query_weight, preferred_element_type=jnp.float32).astype(jnp.bfloat16)
    queries = queries.reshape(pair_count, slot_count, head_local, HEAD_DIM)
    keys_local = (
        jnp.dot(context, key_weight, preferred_element_type=jnp.float32)
        .astype(jnp.bfloat16)
        .reshape(pair_count, key_count, features)
    )
    values_local = (
        jnp.dot(context, value_weight, preferred_element_type=jnp.float32)
        .astype(jnp.bfloat16)
        .reshape(pair_count, key_count, features)
    )
    pair_start = lax.axis_index("pair") * pair_count
    wanted = lax.dynamic_slice_in_dim(partners, pair_start, pair_count)
    pieces = in_one_piece((keys_local, values_local), "pair", 0, 1)
    piece_rows = pieces[0].shape[0]
    select = (wanted[:, None] == jnp.arange(piece_rows, dtype=jnp.int32)[None, :]).astype(
        jnp.bfloat16
    )
    key_total = jnp.einsum(
        "pn,nkf->pkf", select, pieces[0], preferred_element_type=jnp.float32
    ).astype(jnp.bfloat16)
    value_total = jnp.einsum(
        "pn,nkf->pkf", select, pieces[1], preferred_element_type=jnp.float32
    ).astype(jnp.bfloat16)
    key_heads = key_total.reshape(pair_count, key_count, head_local, HEAD_DIM)
    value_heads = value_total.reshape(pair_count, key_count, head_local, HEAD_DIM)
    scores = jnp.einsum(
        "pqhd,pkhd->phqk", queries, key_heads, preferred_element_type=jnp.float32
    ) * HEAD_DIM ** (-0.5)
    row_max = jnp.max(scores, axis=-1, keepdims=True)
    lifted = jnp.exp(scores - row_max)
    weights = (lifted / jnp.sum(lifted, axis=-1, keepdims=True)).astype(jnp.bfloat16)
    attended = jnp.einsum(
        "phqk,pkhd->pqhd", weights, value_heads, preferred_element_type=jnp.float32
    ).astype(jnp.bfloat16)
    partial_value = jnp.dot(
        attended.reshape(row_count, features), output_weight, preferred_element_type=jnp.float32
    )
    current_share = lax.dynamic_slice_in_dim(
        current.reshape(row_count, model_width), column_start, share_width, 1
    ).astype(jnp.float32)
    hidden_share = current_share + lax.psum_scatter(
        partial_value, "mp", scatter_dimension=1, tiled=True
    )
    first_moment, second_moment = lax.psum(
        (jnp.sum(hidden_share, axis=1), jnp.sum(hidden_share * hidden_share, axis=1)), "mp"
    )
    row_mean = first_moment / model_width
    row_var = second_moment / model_width - row_mean * row_mean
    normed_share = (
        (hidden_share - row_mean[:, None]) * lax.rsqrt(row_var[:, None] + 1e-06)
    ).astype(jnp.bfloat16)
    mixer_in = gathered_copies(normed_share, "mp", 1)
    expanded = jax.nn.gelu(
        jnp.dot(mixer_in, up_weight, preferred_element_type=jnp.float32), approximate=False
    ).astype(jnp.bfloat16)
    mlp_result = summed_on_arrival(
        jnp.dot(expanded, down_weight, preferred_element_type=jnp.float32).astype(jnp.bfloat16),
        "mp",
        1,
    )
    is_live = (jnp.arange(slot_count, dtype=jnp.int32)[None, :] < counts[:, None]).reshape(
        row_count, 1
    )
    result = jnp.where(is_live, hidden_share + mlp_result, 0.0).astype(jnp.bfloat16)
    return result.reshape(pair_count, slot_count, share_width)


def solution(mesh):
    placed = (
        P("pair", None, None),
        P("pair", None, None),
        P("pair"),
        P(),
        P(None, "mp"),
        P(None, "mp"),
        P(None, "mp"),
        P("mp", None),
        P(None, "mp"),
        P("mp", None),
    )
    return jax.shard_map(
        body, mesh=mesh, in_specs=placed, out_specs=P("pair", None, "mp"), check_vma=False
    )
```

profile of v0, /device:TPU:32, one launch (start us, length us, event | category | flops | bytes accessed | tf_op | source)
XLA Modules:
  0.0 259.3 jit_solution(9681733598899223378)
XLA Ops:
  6.5 0.0 copy-start
  6.5 0.0 all-gather.2.cloned.1.call-start
  6.5 2.0 convert_reduce_fusion.2
  8.6 0.0 copy-done.2
  8.6 1.2 multiply_reduce_fusion.1
  9.8 0.1 copy.78
  9.8 1.4 copy.52
  11.3 0.1 copy.79
  11.4 0.1 rsqrt.27
  11.5 0.1 div.31
  11.6 2.8 %reshape.124 = f32[392,1024]{1,0:T(8,128)} reshape(f32[2,196,1024]{2,1,0:T(8,128)} %copy.52) | data formatting | bytes 3211264 | tf_op jit(solution)/shard_map/reshape | solution.py:73
  14.4 0.0 copy-done.5
  14.4 1.9 convolution_convert_fusion.4
  16.3 0.0 copy-start.1
  16.3 2.0 convolution_convert_fusion.3
  18.4 0.8 pad_maximum_fusion
  19.3 0.0 all-gather.2.cloned.1.call-update
  19.3 0.2 reduce-scatter.2.cloned.1.call-start
  19.5 0.0 copy-done.1
  19.5 1.4 copy.58
  21.0 0.7 convert_reduce_fusion.1
  21.7 0.1 copy.80
  21.7 1.2 multiply_reduce_fusion
  23.0 0.1 copy.81
  23.1 0.1 rsqrt.29
  23.2 0.1 div.34
  23.2 2.8 %reshape.128 = f32[392,1024]{1,0:T(8,128)} reshape(f32[2,196,1024]{2,1,0:T(8,128)} %copy.58) | data formatting | bytes 3211264 | tf_op jit(solution)/shard_map/reshape | solution.py:69
  26.0 2.0 convolution_convert_fusion.2
  28.0 0.2 reshape.136
  28.2 0.0 copy-done.6
  28.2 0.1 dynamic_slice.7
  28.3 113.5 %all-gather.2.cloned.1.call-done = bf16[128,392,256]{2,1,0:T(8,128)(2,1)} async-done(((bf16[2,392,256]{2,1,0:T(8,128)(2,1)}), bf16[128,392,256]{2,1,0:T(8,128)(2,1)}) %all-gather.2.cloned.1.call-update) | async-done | bytes 25690128 | tf_op jit(solution)/shard_map/all_gather | solution.py:12
  141.8 15.3 %fusion.102 = (bf16[128,196,256]{2,1,0:T(8,128)(2,1)S(1)}, bf16[128,196,256]{2,1,0:T(8,128)(2,1)}) fusion(bf16[128,392,256]{2,1,0:T(8,128)(2,1)} %all-gather.2.cloned.1.call-done), kind=kLoop, calls=%fused_computation.129 | loop fusion | bytes 51380224 | tf_op jit(solution)/shard_map/split | solution.py:13
  157.1 2.1 fusion.20
  159.2 0.9 copy.64
  160.1 6.8 %fusion.17 = bf16[2,196,256]{2,0,1:T(2,128)(2,1)S(1)} fusion(bf16[128,196,256]{2,1,0:T(8,128)(2,1)} %get-tuple-element.10, s32[2]{0:T(128)S(1)} %dynamic_slice.7), kind=kOutput, calls=%fused_computation.39 | convolution fusion | flops 25790720 | bytes 13045768 | tf_op jit(solution)/shard_map/pn,nkf->pkf/dot_general | solution.py:97
  166.9 0.9 copy.57
  167.8 2.9 %exponential_reduce_fusion = (f32[2,4,196]{2,1,0:T(4,128)S(1)}, f32[2,4,196,196]{2,3,1,0:T(8,128)}) fusion(bf16[2,196,4,64]{1,3,2,0:T(8,128)(2,1)} %bitcast.35, bf16[2,196,4,64]{3,2,1,0:T(4,128)(2,1)S(1)} %reshape.136), kind=kOutput, calls=%fused_computation.31 | convolution fusion | flops 40260164 | bytes 1636992 | tf_op jit(solution)/shard_map/sub | solution.py:106
  170.7 1.9 fusion.23
  172.6 0.3 copy.67
  172.9 0.2 reshape.131
  173.1 2.6 %fusion.107 = f32[392,1024]{1,0:T(8,128)} fusion(bf16[392,256]{0,1:T(8,128)(2,1)S(1)} %reshape.131, bf16[256,1024]{1,0:T(8,128)(2,1)} %param.17), kind=kOutput, calls=%fused_computation.131 | convolution fusion | flops 205520896 | bytes 2330624 | tf_op jit(solution)/shard_map/dot_general | solution.py:111
  175.7 0.0 reduce-scatter.2.cloned.1.call-update
  175.7 1.1 copy.51
  176.8 1.3 reshape.123
  178.1 0.0 copy-start.4
  178.2 25.1 %reduce-scatter.2.cloned.1.call-done = f32[392,256]{1,0:T(8,128)} async-done(((f32[392,1024]{1,0:T(8,128)}), f32[392,256]{1,0:T(8,128)}) %reduce-scatter.2.cloned.1.call-update) | async-done | bytes 401424 | tf_op jit(solution)/shard_map/reduce_scatter | solution.py:117
  203.2 1.2 fusion.101
  204.5 9.3 %all-reduce = (f32[392]{0:T(512)S(1)}, f32[392]{0:T(512)S(1)}) all-reduce(f32[392]{0:T(512)S(1)} %get-tuple-element.6, f32[392]{0:T(512)S(1)} %get-tuple-element.5), channel_id=1, replica_groups=mesh['pair'=64,'mp'=4] {'mp'}, use_global_device_ids=true, to_apply=%region_10.0 | all-reduce | flops 784 | bytes 6272 | tf_op jit(solution)/shard_map/psum | solution.py:120
  213.7 1.2 multiply_convert_fusion.3
  214.9 0.1 broadcast_in_dim.11
  215.0 12.5 %all_to_all.10 = bf16[4,392,256]{2,1,0:T(8,128)(2,1)S(1)} all-to-all(bf16[4,392,256]{2,1,0:T(8,128)(2,1)S(1)} %broadcast_in_dim.11), channel_id=1, replica_groups=mesh['pair'=64,'mp'=4] {'mp'}, dimensions={0} | all-to-all | bytes 1605632 | tf_op jit(solution)/shard_map/all_to_all | solution.py:24
  227.5 0.0 copy-done.4
  227.5 0.1 copy.77
  227.6 0.0 copy-done
  227.6 7.5 %convolution_convert_fusion = bf16[392,1024]{1,0:T(8,128)(2,1)} fusion(bf16[1024,1024]{1,0:T(8,128)(2,1)S(1)} %copy-done, bf16[392,1024]{1,0:T(8,128)(2,1)S(1)} %bitcast.33, bf16[1024,1024]{1,0:T(8,128)(2,1)} %param.18), kind=kOutput, calls=%fused_computation.34 | convolution fusion | flops 1670660096 | bytes 5799936 | tf_op jit(solution)/shard_map/dot_general | solution.py:133
  235.1 2.1 copy.101
  237.2 3.6 %all-to-all-start.1 = ((bf16[4,392,256]{2,1,0:T(8,128)(2,1)}), bf16[4,392,256]{2,1,0:T(8,128)(2,1)S(1)}, u32[]{:S(2)}, u32[]{:S(2)}) async-start(bf16[4,392,256]{2,1,0:T(8,128)(2,1)} %bitcast.31), calls=%async_computation.2 | async-start | bytes 1605632 | tf_op jit(solution)/shard_map/all_to_all | solution.py:39
  240.9 0.1 iota_compare_fusion
  241.0 0.1 lt.29
  241.1 9.4 %all-to-all-done.1 = bf16[4,392,256]{2,1,0:T(8,128)(2,1)S(1)} async-done(((bf16[4,392,256]{2,1,0:T(8,128)(2,1)}), bf16[4,392,256]{2,1,0:T(8,128)(2,1)S(1)}, u32[]{:S(2)}, u32[]{:S(2)}) %all-to-all-start.1) | async-done | bytes 802848 | tf_op jit(solution)/shard_map/all_to_all | solution.py:39
  250.4 0.1 convert_reduce_fusion
  250.5 1.1 select_convert_fusion
  251.7 0.8 copy.70
  (15 shorter events, 0.2 us)
Async XLA Ops:
  6.5 221.1 %copy-start = (bf16[1024,1024]{1,0:T(8,128)(2,1)S(1)}, bf16[1024,1024]{1,0:T(8,128)(2,1)}, u32[]{:S(2)}) copy-start(bf16[1024,1024]{1,0:T(8,128)(2,1)} %param.19) | copy-start | bytes 6291460
  6.5 2.0 copy-start.2
  6.5 135.3 %all-gather.2.cloned.1.call-start = ((), (), s32[]{:S(2)}) async-start(), calls=%async_computation.3 | async-start | bytes 26091520 | tf_op jit(solution)/shard_map/all_gather | solution.py:12
  11.6 2.8 %copy-start.5 = (bf16[1024,256]{1,0:T(8,128)(2,1)S(1)}, bf16[1024,256]{1,0:T(8,128)(2,1)}, u32[]{:S(2)}) copy-start(bf16[1024,256]{1,0:T(8,128)(2,1)} %param.15) | copy-start | bytes 1572868
  16.3 3.2 %copy-start.1 = (bf16[2,196,1024]{2,0,1:T(2,128)(2,1)S(1)}, bf16[2,196,1024]{2,0,1:T(2,128)(2,1)}, u32[]{:S(2)}) copy-start(bf16[2,196,1024]{2,0,1:T(2,128)(2,1)} %param.10) | copy-start | bytes 2408452
  19.3 183.9 %reduce-scatter.2.cloned.1.call-start = ((), (), s32[]{:S(2)}) async-start(), calls=%async_computation.4 | async-start | bytes 2007040 | tf_op jit(solution)/shard_map/reduce_scatter | solution.py:117
  26.0 2.2 copy-start.6
  178.1 49.3 %copy-start.4 = (bf16[392,1024]{1,0:T(8,128)(2,1)}, bf16[392,1024]{1,0:T(8,128)(2,1)S(1)}, u32[]{:S(2)}) copy-start(bf16[392,1024]{1,0:T(8,128)(2,1)S(1)} %reshape.123) | copy-start | bytes 2408452
  235.1 5.7 %copy-start.7 = (s32[2]{0:T(128)S(1)}, s32[2]{0:T(128)}, u32[]{:S(2)}) copy-start(s32[2]{0:T(128)} %param.12) | copy-start | bytes 28
  237.2 13.3 %copy-start.3 = (f32[392,256]{1,0:T(8,128)S(1)}, f32[392,256]{1,0:T(8,128)}, u32[]{:S(2)}) copy-start(f32[392,256]{1,0:T(8,128)} %reduce-scatter.2.cloned.1.call-done) | copy-start | bytes 1204228
  237.2 13.2 %all-to-all-start.1 = ((bf16[4,392,256]{2,1,0:T(8,128)(2,1)}), bf16[4,392,256]{2,1,0:T(8,128)(2,1)S(1)}, u32[]{:S(2)}, u32[]{:S(2)}) async-start(bf16[4,392,256]{2,1,0:T(8,128)(2,1)} %bitcast.31), calls=%async_computation.2 | async-start | bytes 1605632 | tf_op jit(solution)/shard_map/all_to_all | solution.py:39
Sparse Core Ops, SparseCore 0:
  19.4 122.3 all-gather.1
  175.8 27.3 reduce-scatter.1
where the time goes:
time: 260 us; the launch traced here: 259 us
  waiting for transfers between devices  148 us (57%)
  local copies, waits for them, and re-layouts  32.7 us (13%)
  matrix products  29.7 us (11%)
  blocking collectives  21.8 us (8%)
  between operations  13.6 us (5%)
  other arithmetic  9.63 us (4%)
  starting transfers between devices  3.85 us (1%)
    all_gather x1, waiting for transfers between devices, in_one_piece(): result = lax.all_gather(both, axis, axis=dim, tiled=True)  114 us
    reduce_scatter x1, waiting for transfers between devices, body(): lax.psum_scatter(partial_value, 'mp', scatter_dimension=1, tiled=True)  25.1 us
    split x1, local copies, waits for them, and re-layouts, in_one_piece(): jnp.split(result, [sum(widths[:k]) for k in range(1, len(widths))], axis=...  15.3 us
    all_to_all x1, blocking collectives, sent_to_all(): return lax.all_to_all(copies, axis, split_axis=0, concat_axis=0, tiled=True)  12.5 us
    all_to_all x1, waiting for transfers between devices, summed_on_arrival(): lax.all_to_all(blocks, axis, split_axis=0, concat_axis=0, tiled=True)  9.37 us
    psum x1, blocking collectives, body(): lax.psum((jnp.sum(hidden_share, axis=1), jnp.sum(hidden_share * hidden_sh...  9.25 us
    dot_general x1, matrix products, body(): jnp.dot(expanded, down_weight, preferred_element_type=jnp.float32)  7.54 us
    dot_general x1, matrix products, body(): jnp.einsum('pn,nkf->pkf', select, pieces[1], preferred_element_type=jnp.f...  6.81 us
  transfers between devices with their start and end apart: 3, of which 3 were waited for; matrix products, arithmetic and copies ran while one was open for 4% of the time, Pallas kernels for 0%

commit v1 on v0

--- a/solution.py
+++ b/solution.py
@@ -1,16 +1,193 @@
+import functools
+
 import jax
 import jax.numpy as jnp
 from jax import lax
+from jax.experimental import pallas as pl
+from jax.experimental.pallas import tpu as pltpu
 from jax.sharding import PartitionSpec as P
 
 HEAD_DIM = 64
-
-
-def in_one_piece(arrays, axis, dim, along):
-    widths = [a.shape[along] for a in arrays]
-    both = jnp.concatenate(arrays, axis=along)
-    result = lax.all_gather(both, axis, axis=dim, tiled=True)
-    return tuple(jnp.split(result, [sum(widths[:k]) for k in range(1, len(widths))], axis=along))
+TILE = 16
+LANES = 128
+MESH = pl.DeviceIdType.MESH
+
+
+def exchange_kernel(
+    groups,
+    shards,
+    partners_ref,
+    past_ref,
+    out_ref,
+    spread,
+    sorted_tiles,
+    context,
+    send_one,
+    recv_one,
+    send_two,
+    recv_two,
+    ring_send,
+    ring_recv,
+):
+    slots, rows, width = past_ref.shape
+    share = width // shards
+    halves = share // LANES
+    blocks = rows // TILE
+    kinds = slots * blocks * halves
+    me = lax.axis_index("pair")
+    rank = lax.axis_index("mp")
+    column = rank * share
+    after = lax.rem(rank + 1, shards)
+    before = lax.rem(rank + shards - 1, shards)
+
+    def keeper(kind):
+        return (kind * groups) // kinds
+
+    mine = (me * kinds + groups - 1) // groups
+    keeps = jnp.logical_and(mine < kinds, keeper(mine) == me)
+
+    def place(kind):
+        slot = kind // (blocks * halves)
+        left = kind % (blocks * halves)
+        row = pl.multiple_of((left // halves) * TILE, TILE)
+        lane = pl.multiple_of(column + (left % halves) * LANES, LANES)
+        return slot, pl.ds(row, TILE), pl.ds(lane, LANES)
+
+    barrier = pltpu.get_barrier_semaphore()
+
+    def greet(step, carry):
+        peer = lax.rem(me + 1 + step, groups)
+        pl.semaphore_signal(barrier, inc=1, device_id={"pair": peer}, device_id_type=MESH)
+        return carry
+
+    lax.fori_loop(0, groups - 1, greet, 0)
+    for peer in (after, before):
+        pl.semaphore_signal(barrier, inc=1, device_id={"mp": peer}, device_id_type=MESH)
+    pl.semaphore_wait(barrier, groups + 1)
+
+    first = (me * kinds) // groups
+
+    def spread_one(step, carry):
+        kind = lax.rem(first + step, kinds)
+        target = keeper(kind)
+        slot, row, lane = place(kind)
+
+        @pl.when(target != me)
+        def _():
+            pltpu.make_async_remote_copy(
+                src_ref=past_ref.at[slot, row, lane],
+                dst_ref=spread.at[me],
+                send_sem=send_one,
+                recv_sem=recv_one,
+                device_id={"pair": target},
+                device_id_type=MESH,
+            ).start()
+
+        @pl.when(target == me)
+        def _():
+            spread[me] = past_ref[slot, row, lane]
+
+        return carry
+
+    lax.fori_loop(0, kinds, spread_one, 0)
+
+    @pl.when(keeps)
+    def _():
+        slot, row, lane = place(mine)
+        arrived = spread.at[pl.ds(0, groups - 1)]
+        pltpu.make_async_copy(arrived, arrived, recv_one).wait()
+
+        def sort_one(step, carry):
+            owner = partners_ref[step * slots + slot] // slots
+            sorted_tiles[step] = spread[owner]
+            return carry
+
+        lax.fori_loop(0, groups, sort_one, 0)
+        context[slot, row, lane] = sorted_tiles[me]
+
+        def deliver(step, carry):
+            target = lax.rem(me + 1 + step, groups)
+            pltpu.make_async_remote_copy(
+                src_ref=sorted_tiles.at[target],
+                dst_ref=context.at[slot, row, lane],
+                send_sem=send_two,
+                recv_sem=recv_two,
+                device_id={"pair": target},
+                device_id_type=MESH,
+            ).start()
+            return carry
+
+        lax.fori_loop(0, groups - 1, deliver, 0)
+        left = spread.at[pl.ds(0, kinds - 1)]
+        pltpu.make_async_copy(left, left, send_one).wait()
+        got = spread.at[pl.ds(0, kinds - 1)]
+        pltpu.make_async_copy(got, got, recv_two).wait()
+        sent = spread.at[pl.ds(0, groups - 1)]
+        pltpu.make_async_copy(sent, sent, send_two).wait()
+
+    @pl.when(jnp.logical_not(keeps))
+    def _():
+        left = spread.at[pl.ds(0, kinds)]
+        pltpu.make_async_copy(left, left, send_one).wait()
+        got = spread.at[pl.ds(0, kinds)]
+        pltpu.make_async_copy(got, got, recv_two).wait()
+
+    def ring(index, owner, slot, peer):
+        part = context.at[slot, :, pl.ds(pl.multiple_of(owner * share, LANES), share)]
+        return pltpu.make_async_remote_copy(
+            src_ref=part,
+            dst_ref=part,
+            send_sem=ring_send.at[index],
+            recv_sem=ring_recv.at[index],
+            device_id={"mp": peer},
+            device_id_type=MESH,
+        )
+
+    up_first, up_second = ring(0, rank, 0, after), ring(1, rank, 1, after)
+    down_first, down_second = ring(2, rank, 1, before), ring(3, rank, 0, before)
+    up_first.start()
+    down_first.start()
+    up_second.start()
+    down_second.start()
+    up_pass, down_pass = ring(4, before, 0, after), ring(5, after, 1, before)
+    up_first.wait_recv()
+    up_pass.start()
+    down_first.wait_recv()
+    down_pass.start()
+    up_second.wait_recv()
+    down_second.wait_recv()
+    up_pass.wait_recv()
+    down_pass.wait_recv()
+    for copy in (up_first, up_second, down_first, down_second, up_pass, down_pass):
+        copy.wait_send()
+    out_ref[...] = context[...]
+
+
+def exchange(partners, past, groups, shards):
+    slots, rows, width = past.shape
+    kinds = slots * (rows // TILE) * (width // shards // LANES)
+    return pl.pallas_call(
+        functools.partial(exchange_kernel, groups, shards),
+        out_shape=jax.ShapeDtypeStruct(past.shape, past.dtype),
+        in_specs=[
+            pl.BlockSpec(memory_space=pltpu.SMEM),
+            pl.BlockSpec(memory_space=pltpu.VMEM),
+        ],
+        out_specs=pl.BlockSpec(memory_space=pltpu.VMEM),
+        scratch_shapes=[
+            pltpu.VMEM((groups, TILE, LANES), past.dtype),
+            pltpu.VMEM((groups, TILE, LANES), past.dtype),
+            pltpu.VMEM(past.shape, past.dtype),
+            pltpu.SemaphoreType.DMA,
+            pltpu.SemaphoreType.DMA,
+            pltpu.SemaphoreType.DMA,
+            pltpu.SemaphoreType.DMA,
+            pltpu.SemaphoreType.DMA((6,)),
+            pltpu.SemaphoreType.DMA((6,)),
+        ],
+        compiler_params=pltpu.CompilerParams(collective_id=0, has_side_effects=True),
+        name="exchange",
+    )(partners, past)
 
 
 def laid_out(blocks, dim):
@@ -69,8 +246,15 @@
     normed = layer_norm(current.astype(jnp.float32).reshape(row_count, model_width)).astype(
         jnp.bfloat16
     )
+    padded = -(-key_count // TILE) * TILE
+    fetched = exchange(
+        partners,
+        jnp.pad(past_tokens, ((0, 0), (0, padded - key_count), (0, 0))),
+        lax.axis_size("pair"),
+        shards,
+    )[:, :key_count]
     context = layer_norm(
-        past_tokens.astype(jnp.float32).reshape(pair_count * key_count, model_width)
+        fetched.astype(jnp.float32).reshape(pair_count * key_count, model_width)
     ).astype(jnp.bfloat16)
     queries = jnp.dot(normed, query_weight, preferred_element_type=jnp.float32).astype(jnp.bfloat16)
     queries = queries.reshape(pair_count, slot_count, head_local, HEAD_DIM)
@@ -84,21 +268,8 @@
         .astype(jnp.bfloat16)
         .reshape(pair_count, key_count, features)
     )
-    pair_start = lax.axis_index("pair") * pair_count
-    wanted = lax.dynamic_slice_in_dim(partners, pair_start, pair_count)
-    pieces = in_one_piece((keys_local, values_local), "pair", 0, 1)
-    piece_rows = pieces[0].shape[0]
-    select = (wanted[:, None] == jnp.arange(piece_rows, dtype=jnp.int32)[None, :]).astype(
-        jnp.bfloat16
-    )
-    key_total = jnp.einsum(
-        "pn,nkf->pkf", select, pieces[0], preferred_element_type=jnp.float32
-    ).astype(jnp.bfloat16)
-    value_total = jnp.einsum(
-        "pn,nkf->pkf", select, pieces[1], preferred_element_type=jnp.float32
-    ).astype(jnp.bfloat16)
-    key_heads = key_total.reshape(pair_count, key_count, head_local, HEAD_DIM)
-    value_heads = value_total.reshape(pair_count, key_count, head_local, HEAD_DIM)
+    key_heads = keys_local.reshape(pair_count, key_count, head_local, HEAD_DIM)
+    value_heads = values_local.reshape(pair_count, key_count, head_local, HEAD_DIM)
     scores = jnp.einsum(
         "pqhd,pkhd->phqk", queries, key_heads, preferred_element_type=jnp.float32
     ) * HEAD_DIM ** (-0.5)

time: 260 us -> 161 us (0.62)
  waiting for transfers between devices: 148 us -> 33.2 us
  Pallas kernels: 0 us -> 39.3 us
  local copies, waits for them, and re-layouts: 32.7 us -> 17.4 us
  matrix products: 29.7 us -> 19.3 us
    all_gather x1 -> x0, waiting for transfers between devices: 114 us -> none  [in_one_piece(): result = lax.all_gather(both, axis, axis=dim, tiled=True)]
    pallas_call x0 -> x1, Pallas kernels: none -> 39.3 us  [exchange(): pl.pallas_call(functools.partial(exchange_kernel, groups, shards), out_sh...]
    split x1 -> x0, local copies, waits for them, and re-layouts: 15.3 us -> none  [in_one_piece(): jnp.split(result, [sum(widths[:k]) for k in range(1, len(widths))], axis=...]
    dot_general x2 -> x0, matrix products: 8.89 us -> none  [the longest x1 6.81 us: body(): jnp.einsum('pn,nkf->pkf', select, pieces[1], preferred_element_type=jnp.f...]
    convert_element_type x3 -> x0, local copies, waits for them, and re-layouts: 3.24 us -> none  [the longest x1 1.45 us: body(): past_tokens.astype(jnp.float32).reshape(pair_count * key_count, model_width)]
  transfers between devices with their start and end apart: 3 -> 2, of which waited for: 3 -> 2; matrix products, arithmetic and copies ran while one was open for 4% -> 2% of each run, Pallas kernels for 0% -> 0%
where the time goes in v1:
time: 161 us; the launch traced here: 160 us
  Pallas kernels  39.3 us (24%)
  waiting for transfers between devices  33.2 us (21%)
  blocking collectives  21.9 us (14%)
  matrix products  19.3 us (12%)
  local copies, waits for them, and re-layouts  17.4 us (11%)
  between operations  13.6 us (8%)
  other arithmetic  11.2 us (7%)
  starting transfers between devices  3.63 us (2%)
    pallas_call x1, Pallas kernels, exchange(): pl.pallas_call(functools.partial(exchange_kernel, groups, shards), out_sh...  39.3 us
    reduce_scatter x1, waiting for transfers between devices, body(): lax.psum_scatter(partial_value, 'mp', scatter_dimension=1, tiled=True)  23.8 us
    all_to_all x1, blocking collectives, sent_to_all(): return lax.all_to_all(copies, axis, split_axis=0, concat_axis=0, tiled=True)  12.7 us
    all_to_all x1, waiting for transfers between devices, summed_on_arrival(): lax.all_to_all(blocks, axis, split_axis=0, concat_axis=0, tiled=True)  9.37 us
    psum x1, blocking collectives, body(): lax.psum((jnp.sum(hidden_share, axis=1), jnp.sum(hidden_share * hidden_sh...  9.3 us
    dot_general x1, matrix products, body(): jnp.dot(expanded, down_weight, preferred_element_type=jnp.float32)  7.54 us
    all_to_all x1, starting transfers between devices, summed_on_arrival(): lax.all_to_all(blocks, axis, split_axis=0, concat_axis=0, tiled=True)  3.63 us
    reduce_sum x2, other arithmetic, layer_norm(): center = values - jnp.mean(values, axis=-1, keepdims=True)  3.41 us
  transfers between devices with their start and end apart: 2, of which 2 were waited for; matrix products, arithmetic and copies ran while one was open for 2% of the time, Pallas kernels for 0%

profile of v1, /device:TPU:32, one launch (start us, length us, event | category | flops | bytes accessed | tf_op | source)
XLA Modules:
  0.0 159.6 jit_solution(9094346312417514242)
XLA Ops:
  6.5 0.0 copy-start
  6.5 0.0 reduce-scatter.2.cloned.1.call-start
  6.5 2.0 %convert_reduce_fusion.2 = f32[2,196]{0,1:T(8,128)S(1)} fusion(bf16[2,196,1024]{2,0,1:T(2,128)(2,1)} %param.10), kind=kLoop, calls=%fused_computation.71 | loop fusion | flops 802424 | bytes 804384 | tf_op jit(solution)/shard_map/reduce_sum | solution.py:221
  8.6 0.1 copy.92
  8.6 0.0 copy-done.3
  8.6 1.2 multiply_reduce_fusion.1
  9.8 1.3 copy.67
  11.2 1.0 pad.4.past_ref
  12.2 39.3 %exchange.1 = bf16[2,208,1024]{2,1,0:T(8,128)(2,1)} custom-call(s32[128]{0:T(128)} %partners_ref.1, bf16[2,208,1024]{2,1,0:T(8,128)(2,1)} %pad.4.past_ref), custom_call_target="tpu_custom_call" | custom-call | tf_op jit(solution)/shard_map/exchange/pallas_call | solution.py:169
  51.4 0.0 copy-start.2
  51.5 1.4 convert_reduce_fusion.1
  52.9 0.1 div.31
  53.0 1.6 multiply_reduce_fusion
  54.5 0.0 copy-done.2
  54.5 1.4 slice_convert_fusion
  55.9 0.0 copy-done.4
  55.9 1.4 copy.69
  57.4 0.1 copy.93
  57.4 0.1 rsqrt.29
  57.5 0.1 div.34
  57.6 0.1 rsqrt.27
  57.7 2.8 %reshape.111 = f32[392,1024]{1,0:T(8,128)} reshape(f32[2,196,1024]{2,1,0:T(8,128)} %slice_convert_fusion) | data formatting | bytes 3211264 | tf_op jit(solution)/shard_map/reshape | solution.py:257
  60.5 0.0 copy-done.8
  60.6 2.0 %convolution_convert_fusion.2 = bf16[392,256]{1,0:T(8,128)(2,1)S(1)} fusion(bf16[1024,256]{1,0:T(8,128)(2,1)S(1)} %copy-done.8, f32[392,1024]{1,0:T(8,128)} %reshape.111, f32[392]{0:T(512)S(1)} %rsqrt.27, f32[392]{0:T(512)S(1)} %div.31), kind=kOutput, calls=%fused_computation.32 | convolution fusion | flops 206825472 | bytes 2333760 | tf_op jit(solution)/shard_map/dot_general | solution.py:262
  62.6 0.0 copy-done.1
  62.6 0.0 copy-done.9
  62.6 0.5 convolution_convert_fusion.4
  63.1 0.2 reshape.118
  63.3 1.0 reshape.120
  64.2 2.8 %reshape.112 = f32[392,1024]{1,0:T(8,128)} reshape(f32[2,196,1024]{2,1,0:T(8,128)} %copy.69) | data formatting | bytes 3211264 | tf_op jit(solution)/shard_map/reshape | solution.py:246
  67.0 0.0 copy-done.10
  67.1 1.9 %convolution_convert_fusion.3 = bf16[392,256]{1,0:T(8,128)(2,1)S(1)} fusion(bf16[1024,256]{1,0:T(8,128)(2,1)S(1)} %copy-done.10, f32[392,1024]{1,0:T(8,128)} %reshape.112, f32[392]{0:T(512)S(1)} %rsqrt.29, f32[392]{0:T(512)S(1)} %div.34), kind=kOutput, calls=%fused_computation.33 | convolution fusion | flops 206825472 | bytes 2333760 | tf_op jit(solution)/shard_map/dot_general | solution.py:259
  68.9 0.2 reshape.119
  69.1 2.9 %exponential_reduce_fusion = (f32[2,4,196]{2,1,0:T(4,128)S(1)}, f32[2,4,196,196]{2,3,1,0:T(8,128)}) fusion(bf16[2,196,4,64]{3,2,1,0:T(4,128)(2,1)} %reshape.120, bf16[2,196,4,64]{3,2,1,0:T(4,128)(2,1)S(1)} %reshape.119), kind=kOutput, calls=%fused_computation.27 | convolution fusion | flops 40260164 | bytes 1636992 | tf_op jit(solution)/shard_map/sub | solution.py:277
  72.0 1.9 %fusion.13 = bf16[2,196,4,64]{1,3,2,0:T(8,128)(2,1)S(1)} fusion(f32[2,4,196,196]{2,3,1,0:T(8,128)} %get-tuple-element.12, f32[2,4,196]{2,1,0:T(4,128)S(1)} %get-tuple-element.11, bf16[2,196,4,64]{3,2,1,0:T(4,128)(2,1)S(1)} %reshape.118), kind=kOutput, calls=%fused_computation.35 | convolution fusion | flops 40052992 | bytes 1636992 | tf_op jit(solution)/shard_map/phqk,pkhd->pqhd/dot_general | solution.py:279
  73.9 0.3 copy.79
  74.2 0.2 reshape.114
  74.4 0.0 copy-start.5
  74.4 2.7 %fusion.102 = f32[392,1024]{1,0:T(8,128)} fusion(bf16[392,256]{0,1:T(8,128)(2,1)S(1)} %reshape.114, bf16[256,1024]{1,0:T(8,128)(2,1)} %param.17), kind=kOutput, calls=%fused_computation.121 | convolution fusion | flops 205520896 | bytes 2330624 | tf_op jit(solution)/shard_map/dot_general | solution.py:282
  77.1 0.0 reduce-scatter.2.cloned.1.call-update
  77.1 0.0 copy-done.5
  77.1 1.1 copy.66
  78.2 1.3 reshape.110
  79.5 0.0 copy-start.7
  79.5 23.8 %reduce-scatter.2.cloned.1.call-done = f32[392,256]{1,0:T(8,128)} async-done(((f32[392,1024]{1,0:T(8,128)}), f32[392,256]{1,0:T(8,128)}) %reduce-scatter.2.cloned.1.call-update) | async-done | bytes 401424 | tf_op jit(solution)/shard_map/reduce_scatter | solution.py:288
  103.3 1.2 fusion.95
  104.5 9.3 %all-reduce.1 = (f32[392]{0:T(512)S(1)}, f32[392]{0:T(512)S(1)}) all-reduce(f32[392]{0:T(512)S(1)} %get-tuple-element.6, f32[392]{0:T(512)S(1)} %get-tuple-element.5), channel_id=1, replica_groups=mesh['pair'=64,'mp'=4] {'mp'}, use_global_device_ids=true, to_apply=%region_10.11 | all-reduce | flops 784 | bytes 6272 | tf_op jit(solution)/shard_map/psum | solution.py:291
  113.8 1.2 multiply_convert_fusion.3
  115.0 0.1 broadcast_in_dim.11
  115.1 12.7 %all_to_all.10 = bf16[4,392,256]{2,1,0:T(8,128)(2,1)S(1)} all-to-all(bf16[4,392,256]{2,1,0:T(8,128)(2,1)S(1)} %broadcast_in_dim.11), channel_id=1, replica_groups=mesh['pair'=64,'mp'=4] {'mp'}, dimensions={0} | all-to-all | bytes 1605632 | tf_op jit(solution)/shard_map/all_to_all | solution.py:201
  127.7 0.0 copy-done.7
  127.7 0.1 copy.91
  127.8 0.0 copy-done
  127.8 7.5 %convolution_convert_fusion = bf16[392,1024]{1,0:T(8,128)(2,1)} fusion(bf16[1024,1024]{1,0:T(8,128)(2,1)S(1)} %copy-done, bf16[392,1024]{1,0:T(8,128)(2,1)S(1)} %bitcast.24, bf16[1024,1024]{1,0:T(8,128)(2,1)} %param.18), kind=kOutput, calls=%fused_computation.30 | convolution fusion | flops 1670660096 | bytes 5799936 | tf_op jit(solution)/shard_map/dot_general | solution.py:304
  135.4 2.1 %copy.117 = bf16[49,4,8,256]{3,2,0,1:T(8,128)(2,1)} copy(bf16[49,4,8,256]{3,2,1,0:T(8,128)(2,1)} %bitcast.25) | data formatting | bytes 1605632 | tf_op jit(solution)/shard_map/reshape | solution.py:210
  137.5 3.6 %all-to-all-start.1 = ((bf16[4,392,256]{2,1,0:T(8,128)(2,1)}), bf16[4,392,256]{2,1,0:T(8,128)(2,1)S(1)}, u32[]{:S(2)}, u32[]{:S(2)}) async-start(bf16[4,392,256]{2,1,0:T(8,128)(2,1)} %bitcast.22), calls=%async_computation.2 | async-start | bytes 1605632 | tf_op jit(solution)/shard_map/all_to_all | solution.py:216
  141.1 0.0 copy-done.11
  141.1 0.1 iota_compare_fusion
  141.2 0.1 lt.26
  141.3 9.4 %all-to-all-done.1 = bf16[4,392,256]{2,1,0:T(8,128)(2,1)S(1)} async-done(((bf16[4,392,256]{2,1,0:T(8,128)(2,1)}), bf16[4,392,256]{2,1,0:T(8,128)(2,1)S(1)}, u32[]{:S(2)}, u32[]{:S(2)}) %all-to-all-start.1) | async-done | bytes 802848 | tf_op jit(solution)/shard_map/all_to_all | solution.py:216
  150.7 0.1 convert_reduce_fusion
  150.8 0.0 copy-done.6
  150.8 1.1 select_convert_fusion
  151.9 0.8 copy.82
  (14 shorter events, 0.1 us)
Async XLA Ops:
  6.5 121.3 %copy-start = (bf16[1024,1024]{1,0:T(8,128)(2,1)S(1)}, bf16[1024,1024]{1,0:T(8,128)(2,1)}, u32[]{:S(2)}) copy-start(bf16[1024,1024]{1,0:T(8,128)(2,1)} %param.19) | copy-start | bytes 6291460
  6.5 2.1 %copy-start.3 = (bf16[2,196,1024]{2,0,1:T(2,128)(2,1)S(1)}, bf16[2,196,1024]{2,0,1:T(2,128)(2,1)}, u32[]{:S(2)}) copy-start(bf16[2,196,1024]{2,0,1:T(2,128)(2,1)} %param.10) | copy-start | bytes 2408452
  6.5 96.8 %reduce-scatter.2.cloned.1.call-start = ((), (), s32[]{:S(2)}) async-start(), calls=%async_computation.3 | async-start | bytes 2007040 | tf_op jit(solution)/shard_map/reduce_scatter | solution.py:288
  51.4 3.1 %copy-start.2 = (bf16[2,208,1024]{2,1,0:T(8,128)(2,1)S(1)}, bf16[2,208,1024]{2,1,0:T(8,128)(2,1)}, u32[]{:S(2)}) copy-start(bf16[2,208,1024]{2,1,0:T(8,128)(2,1)} %exchange.1) | copy-start | bytes 2555908
  53.0 3.0 %copy-start.4 = (bf16[2,196,1024]{2,0,1:T(2,128)(2,1)S(1)}, bf16[2,196,1024]{2,0,1:T(2,128)(2,1)}, u32[]{:S(2)}) copy-start(bf16[2,196,1024]{2,0,1:T(2,128)(2,1)} %param.10) | copy-start | bytes 2408452
  57.7 2.8 %copy-start.8 = (bf16[1024,256]{1,0:T(8,128)(2,1)S(1)}, bf16[1024,256]{1,0:T(8,128)(2,1)}, u32[]{:S(2)}) copy-start(bf16[1024,256]{1,0:T(8,128)(2,1)} %param.15) | copy-start | bytes 1572868
  60.5 2.0 %copy-start.1 = (f32[392,1024]{1,0:T(8,128)S(1)}, f32[392,1024]{1,0:T(8,128)}, u32[]{:S(2)}) copy-start(f32[392,1024]{1,0:T(8,128)} %reshape.111) | copy-start | bytes 4816900
  60.6 2.0 %copy-start.9 = (bf16[1024,256]{1,0:T(8,128)(2,1)S(1)}, bf16[1024,256]{1,0:T(8,128)(2,1)}, u32[]{:S(2)}) copy-start(bf16[1024,256]{1,0:T(8,128)(2,1)} %param.16) | copy-start | bytes 1572868
  64.2 2.8 %copy-start.10 = (bf16[1024,256]{1,0:T(8,128)(2,1)S(1)}, bf16[1024,256]{1,0:T(8,128)(2,1)}, u32[]{:S(2)}) copy-start(bf16[1024,256]{1,0:T(8,128)(2,1)} %param.14) | copy-start | bytes 1572868
  74.4 2.7 %copy-start.5 = (bf16[2,196,1024]{2,0,1:T(2,128)(2,1)S(1)}, bf16[2,196,1024]{2,0,1:T(2,128)(2,1)}, u32[]{:S(2)}) copy-start(bf16[2,196,1024]{2,0,1:T(2,128)(2,1)} %param.10) | copy-start | bytes 2408452
  79.5 48.2 %copy-start.7 = (bf16[392,1024]{1,0:T(8,128)(2,1)}, bf16[392,1024]{1,0:T(8,128)(2,1)S(1)}, u32[]{:S(2)}) copy-start(bf16[392,1024]{1,0:T(8,128)(2,1)S(1)} %reshape.110) | copy-start | bytes 2408452
  135.4 5.7 %copy-start.11 = (s32[2]{0:T(128)S(1)}, s32[2]{0:T(128)}, u32[]{:S(2)}) copy-start(s32[2]{0:T(128)} %param.12) | copy-start | bytes 28
  137.5 13.3 %copy-start.6 = (f32[392,256]{1,0:T(8,128)S(1)}, f32[392,256]{1,0:T(8,128)}, u32[]{:S(2)}) copy-start(f32[392,256]{1,0:T(8,128)} %reduce-scatter.2.cloned.1.call-done) | copy-start | bytes 1204228
  137.5 13.2 %all-to-all-start.1 = ((bf16[4,392,256]{2,1,0:T(8,128)(2,1)}), bf16[4,392,256]{2,1,0:T(8,128)(2,1)S(1)}, u32[]{:S(2)}, u32[]{:S(2)}) async-start(bf16[4,392,256]{2,1,0:T(8,128)(2,1)} %bitcast.22), calls=%async_computation.2 | async-start | bytes 1605632 | tf_op jit(solution)/shard_map/all_to_all | solution.py:216
Sparse Core Ops, SparseCore 0:
  77.2 26.0 reduce-scatter.1

commit v2 on v1

v2 whole, which is shorter than its diff:
```python
import functools

import jax
import jax.numpy as jnp
from jax import lax
from jax.experimental import pallas as pl
from jax.experimental.pallas import tpu as pltpu
from jax.sharding import PartitionSpec as P

HEAD_DIM = 64
TILE = 16
LANES = 128
MESH = pl.DeviceIdType.MESH
F32 = jnp.float32
BF16 = jnp.bfloat16


class Ring:
    def __init__(self, part, rank, after, before, send, recv, base):
        def copy(index, owner, half, peer):
            ref = part(owner, half)
            return pltpu.make_async_remote_copy(
                src_ref=ref,
                dst_ref=ref,
                send_sem=send.at[base + index],
                recv_sem=recv.at[base + index],
                device_id={"mp": peer},
                device_id_type=MESH,
            )

        self.up = (copy(0, rank, 0, after), copy(1, rank, 1, after), copy(2, before, 0, after))
        self.down = (copy(3, rank, 1, before), copy(4, rank, 0, before), copy(5, after, 1, before))

    def start(self, step):
        self.up[step].start()
        self.down[step].start()

    def forward(self):
        self.up[0].wait_recv()
        self.up[2].start()
        self.down[0].wait_recv()
        self.down[2].start()

    def arrive(self):
        for step in (1, 2):
            self.up[step].wait_recv()
            self.down[step].wait_recv()

    def settle(self):
        for copy in self.up + self.down:
            copy.wait_send()


def normalize(source, target, rows):
    for first in range(0, rows, TILE):
        values = source[first : first + TILE, :].astype(F32)
        center = values - jnp.mean(values, axis=-1, keepdims=True)
        spread = jnp.mean(center * center, axis=-1, keepdims=True)
        target[first : first + TILE, :] = (center * lax.rsqrt(spread + 1e-06)).astype(BF16)


def gelu(values):
    return 0.5 * values * (1.0 + lax.erf(values * (0.5**0.5)))


def decoder_kernel(
    groups,
    shards,
    keys,
    partners_ref,
    past_hbm,
    current_hbm,
    query_hbm,
    key_hbm,
    value_hbm,
    output_hbm,
    up_hbm,
    down_hbm,
    out_ref,
    past,
    current,
    query_weight,
    key_weight,
    value_weight,
    output_weight,
    up_weight,
    down_weight,
    spread,
    sorted_tiles,
    context,
    normed,
    queries,
    attended,
    hidden,
    partial,
    packed,
    summed,
    landed,
    load,
    exchange_sem,
    ring_send,
    ring_recv,
):
    slots, rows, width = past.shape
    share = width // shards
    halves = share // LANES
    blocks = rows // TILE
    kinds = slots * blocks * halves
    me = lax.axis_index("pair")
    rank = lax.axis_index("mp")
    column = pl.multiple_of(rank * share, LANES)
    after = lax.rem(rank + 1, shards)
    before = lax.rem(rank + shards - 1, shards)
    across = lax.rem(rank + 2, shards)
    core = lax.rem(me, 2)
    twin = me + 1 - 2 * core

    def fetch(index, source, target):
        copy = pltpu.make_async_copy(source, target, load.at[index])
        copy.start()
        return copy

    get_output = fetch(
        0, output_hbm, output_weight.at[pl.ds(pl.multiple_of(rank * share, share), share), :]
    )
    get_past = fetch(1, past_hbm, past)
    get_current = fetch(2, current_hbm, current)
    get_query = fetch(3, query_hbm, query_weight)
    get_key = fetch(4, key_hbm, key_weight)
    get_value = fetch(5, value_hbm, value_weight)
    get_up = fetch(6, up_hbm, up_weight)
    get_down = fetch(7, down_hbm, down_weight)

    def keeper(kind):
        return (kind * groups) // kinds

    mine = (me * kinds + groups - 1) // groups
    keeps = jnp.logical_and(mine < kinds, keeper(mine) == me)

    def place(kind):
        slot = kind // (blocks * halves)
        left = kind % (blocks * halves)
        row = pl.multiple_of((left // halves) * TILE, TILE)
        lane = pl.multiple_of(column + (left % halves) * LANES, LANES)
        return slot, pl.ds(row, TILE), pl.ds(lane, LANES)

    barrier = pltpu.get_barrier_semaphore()

    def greet(step, carry):
        peer = lax.rem(me + 1 + step, groups)
        pl.semaphore_signal(barrier, inc=1, device_id={"pair": peer}, device_id_type=MESH)
        return carry

    lax.fori_loop(0, groups - 1, greet, 0)
    for peer in (after, before):
        pl.semaphore_signal(barrier, inc=1, device_id={"mp": peer}, device_id_type=MESH)
    pl.semaphore_wait(barrier, groups + 1)

    get_past.wait()
    first = (me * kinds) // groups

    def spread_one(step, carry):
        kind = lax.rem(first + step, kinds)
        target = keeper(kind)
        slot, row, lane = place(kind)

        @pl.when(target != me)
        def _():
            pltpu.make_async_remote_copy(
                src_ref=past.at[slot, row, lane],
                dst_ref=spread.at[me],
                send_sem=exchange_sem.at[0],
                recv_sem=exchange_sem.at[1],
                device_id={"pair": target},
                device_id_type=MESH,
            ).start()

        @pl.when(target == me)
        def _():
            spread[me] = past[slot, row, lane]

        return carry

    lax.fori_loop(0, kinds, spread_one, 0)

    half = share // 2
    quarter = half // 2

    def weight_rows(owner, piece):
        row = pl.multiple_of(owner * share + core * half + piece * quarter, quarter)
        return output_weight.at[pl.ds(row, quarter), :]

    weight_ring = Ring(weight_rows, rank, after, before, ring_send, ring_recv, 0)
    get_output.wait()
    weight_ring.start(0)
    weight_ring.start(1)

    get_current.wait()
    get_query.wait()
    for slot in range(slots):
        normalize(current.at[slot], normed, rows)
        queries[slot] = jnp.dot(
            normed[...], query_weight[...], preferred_element_type=F32
        ).astype(BF16)

    @pl.when(keeps)
    def _():
        slot, row, lane = place(mine)
        arrived = spread.at[pl.ds(0, groups - 1)]
        pltpu.make_async_copy(arrived, arrived, exchange_sem.at[1]).wait()

        def sort_one(step, carry):
            owner = partners_ref[step * slots + slot] // slots
            sorted_tiles[step] = spread[owner]
            return carry

        lax.fori_loop(0, groups, sort_one, 0)
        context[slot, row, lane] = sorted_tiles[me]

        def deliver(step, carry):
            target = lax.rem(me + 1 + step, groups)
            pltpu.make_async_remote_copy(
                src_ref=sorted_tiles.at[target],
                dst_ref=context.at[slot, row, lane],
                send_sem=exchange_sem.at[2],
                recv_sem=exchange_sem.at[3],
                device_id={"pair": target},
                device_id_type=MESH,
            ).start()
            return carry

        lax.fori_loop(0, groups - 1, deliver, 0)

    weight_ring.forward()

    @pl.when(keeps)
    def _():
        got = spread.at[pl.ds(0, kinds - 1)]
        pltpu.make_async_copy(got, got, exchange_sem.at[3]).wait()

    @pl.when(jnp.logical_not(keeps))
    def _():
        got = spread.at[pl.ds(0, kinds)]
        pltpu.make_async_copy(got, got, exchange_sem.at[3]).wait()

    def columns_of(buffer, slot):
        def part(owner, piece):
            lane = pl.multiple_of(owner * share + piece * LANES, LANES)
            return buffer.at[slot, :, pl.ds(lane, LANES)]

        return part

    context_rings = [
        Ring(columns_of(context, slot), rank, after, before, ring_send, ring_recv, 6 + 6 * slot)
        for slot in range(slots)
    ]
    attended_rings = [
        Ring(columns_of(attended, slot), rank, after, before, ring_send, ring_recv, 18 + 6 * slot)
        for slot in range(slots)
    ]
    context_rings[0].start(0)
    context_rings[0].start(1)
    context_rings[1].start(0)
    weight_ring.arrive()

    def to_twin(index, owner):
        row = pl.multiple_of(owner * share + core * half, half)
        ref = output_weight.at[pl.ds(row, half), :]
        return pltpu.make_async_remote_copy(
            src_ref=ref,
            dst_ref=ref,
            send_sem=ring_send.at[30 + index],
            recv_sem=ring_recv.at[30 + index],
            device_id={"pair": twin},
            device_id_type=MESH,
        )

    twins = [to_twin(index, owner) for index, owner in enumerate((before, after, across))]
    for copy in twins:
        copy.start()
    context_rings[0].forward()
    context_rings[1].start(1)

    lanes = lax.broadcasted_iota(jnp.int32, (rows, share), 1) // HEAD_DIM
    seen = lax.broadcasted_iota(jnp.int32, (rows, rows), 1) < keys

    def attend(slot):
        normalize(context.at[slot], normed, rows)
        key = jnp.dot(normed[...], key_weight[...], preferred_element_type=F32).astype(BF16)
        value = jnp.dot(normed[...], value_weight[...], preferred_element_type=F32).astype(BF16)
        query = queries[slot]
        total = jnp.zeros((rows, share), F32)
        for head in range(share // HEAD_DIM):
            one = jnp.where(lanes == head, query, jnp.zeros_like(query))
            scores = (
                lax.dot_general(one, key, (((1,), (1,)), ((), ())), preferred_element_type=F32)
                * HEAD_DIM ** (-0.5)
            )
            scores = jnp.where(seen, scores, -jnp.inf)
            lifted = jnp.exp(scores - jnp.max(scores, axis=-1, keepdims=True))
            weights = (lifted * (1.0 / jnp.sum(lifted, axis=-1, keepdims=True))).astype(BF16)
            total = jnp.where(
                lanes == head, jnp.dot(weights, value, preferred_element_type=F32), total
            )
        attended[slot, :, pl.ds(column, share)] = total.astype(BF16)

    get_key.wait()
    get_value.wait()
    context_rings[0].arrive()
    attend(0)
    attended_rings[0].start(0)
    attended_rings[0].start(1)
    context_rings[1].forward()
    context_rings[1].arrive()
    attended_rings[0].forward()
    attend(1)
    attended_rings[1].start(0)
    attended_rings[1].start(1)

    def block(owner, piece):
        return pl.ds(pl.multiple_of(owner * share + piece * LANES, LANES), LANES)

    def sends(slot):
        base = 33 + 6 * slot

        def copy(index, source, target, peer):
            return pltpu.make_async_remote_copy(
                src_ref=source,
                dst_ref=target,
                send_sem=ring_send.at[base + index],
                recv_sem=ring_recv.at[base + index],
                device_id={"mp": peer},
                device_id_type=MESH,
            )

        return [
            copy(0, packed.at[slot, :, block(across, 0)], landed.at[slot, 0], after),
            copy(1, packed.at[slot, :, block(across, 1)], landed.at[slot, 1], before),
            copy(2, packed.at[slot, :, block(after, 1)], landed.at[slot, 2], after),
            copy(3, packed.at[slot, :, block(before, 0)], landed.at[slot, 3], before),
            copy(4, summed.at[slot, 0], landed.at[slot, 4], after),
            copy(5, summed.at[slot, 1], landed.at[slot, 5], before),
        ]

    reductions = [sends(slot) for slot in range(slots)]

    def mix(slot):
        hidden[slot] = current[slot].astype(F32) + jnp.dot(
            attended[slot], output_weight[...], preferred_element_type=F32
        )
        normalize(hidden.at[slot], normed, rows)
        expanded = gelu(
            jnp.dot(normed[...], up_weight[...], preferred_element_type=F32)
        ).astype(BF16)
        result = jnp.dot(expanded, down_weight[...], preferred_element_type=F32)
        partial[slot] = result
        packed[slot] = result.astype(BF16)
        for copy in reductions[slot][:4]:
            copy.start()

    def relay(slot):
        for piece, owner in ((0, after), (1, before)):
            reductions[slot][piece].wait_recv()
            summed[slot, piece] = (
                partial[slot, :, block(owner, piece)] + landed[slot, piece].astype(F32)
            ).astype(BF16)
            reductions[slot][4 + piece].start()

    def finish(slot):
        for copy in reductions[slot][2:]:
            copy.wait_recv()
        for piece, others in ((0, (4, 3)), (1, (2, 5))):
            mine_at = block(rank, piece)
            result = partial[slot, :, mine_at]
            for other in others:
                result = result + landed[slot, other].astype(F32)
            out_ref[slot, :, piece * LANES : (piece + 1) * LANES] = (
                hidden[slot, :, mine_at] + result
            ).astype(BF16)

    attended_rings[0].arrive()
    for copy in twins:
        copy.wait_recv()
    get_up.wait()
    get_down.wait()
    attended_rings[1].forward()
    mix(0)
    attended_rings[1].arrive()
    relay(0)
    mix(1)
    finish(0)
    relay(1)
    finish(1)

    for ring in [weight_ring] + context_rings + attended_rings:
        ring.settle()
    for copy in twins + reductions[0] + reductions[1]:
        copy.wait_send()

    @pl.when(keeps)
    def _():
        left = spread.at[pl.ds(0, kinds - 1)]
        pltpu.make_async_copy(left, left, exchange_sem.at[0]).wait()
        sent = spread.at[pl.ds(0, groups - 1)]
        pltpu.make_async_copy(sent, sent, exchange_sem.at[2]).wait()

    @pl.when(jnp.logical_not(keeps))
    def _():
        left = spread.at[pl.ds(0, kinds)]
        pltpu.make_async_copy(left, left, exchange_sem.at[0]).wait()


def body(
    current,
    past_tokens,
    counts,
    partners,
    query_weight,
    key_weight,
    value_weight,
    output_weight,
    up_weight,
    down_weight,
):
    pair_count, slot_count, model_width = current.shape
    key_count = past_tokens.shape[1]
    groups, shards = lax.axis_size("pair"), lax.axis_size("mp")
    share = model_width // shards
    features = query_weight.shape[1]
    hidden_units = up_weight.shape[1]
    rows = -(-key_count // TILE) * TILE
    padding = ((0, 0), (0, rows - key_count), (0, 0))
    kinds = pair_count * (rows // TILE) * (share // LANES)
    whole = pl.BlockSpec(memory_space=pl.ANY)
    full = (pair_count, rows, model_width)
    result = pl.pallas_call(
        functools.partial(decoder_kernel, groups, shards, key_count),
        out_shape=jax.ShapeDtypeStruct((pair_count, rows, share), BF16),
        in_specs=[pl.BlockSpec(memory_space=pltpu.SMEM)] + [whole] * 8,
        out_specs=pl.BlockSpec(memory_space=pltpu.VMEM),
        scratch_shapes=[
            pltpu.VMEM(full, BF16),
            pltpu.VMEM(full, BF16),
            pltpu.VMEM((model_width, features), BF16),
            pltpu.VMEM((model_width, features), BF16),
            pltpu.VMEM((model_width, features), BF16),
            pltpu.VMEM((model_width, model_width), BF16),
            pltpu.VMEM((model_width, hidden_units), BF16),
            pltpu.VMEM((hidden_units, model_width), BF16),
            pltpu.VMEM((groups, TILE, LANES), BF16),
            pltpu.VMEM((groups, TILE, LANES), BF16),
            pltpu.VMEM(full, BF16),
            pltpu.VMEM((rows, model_width), BF16),
            pltpu.VMEM((pair_count, rows, features), BF16),
            pltpu.VMEM(full, BF16),
            pltpu.VMEM(full, F32),
            pltpu.VMEM(full, F32),
            pltpu.VMEM(full, BF16),
            pltpu.VMEM((pair_count, 2, rows, LANES), BF16),
            pltpu.VMEM((pair_count, 6, rows, LANES), BF16),
            pltpu.SemaphoreType.DMA((8,)),
            pltpu.SemaphoreType.DMA((4,)),
            pltpu.SemaphoreType.DMA((45,)),
            pltpu.SemaphoreType.DMA((45,)),
        ],
        compiler_params=pltpu.CompilerParams(
            collective_id=0, has_side_effects=True, vmem_limit_bytes=56 * 1024 * 1024
        ),
        name="decoder",
    )(
        partners,
        jnp.pad(past_tokens, padding),
        jnp.pad(current, padding),
        query_weight,
        key_weight,
        value_weight,
        output_weight,
        up_weight,
        down_weight,
    )
    live = jnp.arange(slot_count, dtype=jnp.int32)[None, :, None] < counts[:, None, None]
    return jnp.where(live, result[:, :slot_count], jnp.zeros((), BF16))


def solution(mesh):
    placed = (
        P("pair", None, None),
        P("pair", None, None),
        P("pair"),
        P(),
        P(None, "mp"),
        P(None, "mp"),
        P(None, "mp"),
        P("mp", None),
        P(None, "mp"),
        P("mp", None),
    )
    return jax.shard_map(
        body, mesh=mesh, in_specs=placed, out_specs=P("pair", None, "mp"), check_vma=False
    )
```

time: 161 us -> 72.4 us (0.45)
  the two profiles are of different devices: /device:TPU:32 before, /device:TPU:8 now
where the time goes in v2:
time: 72.4 us; the launch traced here: 72.3 us
  Pallas kernels  66.7 us (92%)
  local copies, waits for them, and re-layouts  4.45 us (6%)
  other arithmetic  1.12 us (2%)
    pallas_call x1, Pallas kernels, body(): pl.pallas_call(functools.partial(decoder_kernel, groups, shards, key_coun...  66.7 us
    unnamed x6, local copies, waits for them, and re-layouts  1.62 us

profile of v2, /device:TPU:8, one launch (start us, length us, event | category | flops | bytes accessed | tf_op | source)
XLA Modules:
  0.0 72.3 jit_solution(4488460162542615952)
XLA Ops:
  0.0 0.0 copy-start
  0.0 1.4 %copy.11 = bf16[2,196,1024]{2,1,0:T(8,128)(2,1)S(1)} copy(bf16[2,196,1024]{2,0,1:T(2,128)(2,1)} %param.11) | data formatting | bytes 1605632 | tf_op args[1]
  1.4 1.0 %pad.7.past_hbm = bf16[2,208,1024]{2,1,0:T(8,128)(2,1)} pad(bf16[2,196,1024]{2,1,0:T(8,128)(2,1)S(1)} %copy.11, bf16[]{:T(256)} %constant.1.clone.1), padding=0_0x0_12x0_0 | pad | bytes 1654786 | tf_op jit(solution)/shard_map/jit(_pad)/pad | solution.py:472
  2.4 0.0 copy-done
  2.4 0.2 copy.12
  2.6 1.0 %pad.8.current_hbm = bf16[2,208,1024]{2,1,0:T(8,128)(2,1)} pad(bf16[2,196,1024]{2,1,0:T(8,128)(2,1)S(1)} %copy.12, bf16[]{:T(256)} %constant.1.clone.1), padding=0_0x0_12x0_0 | pad | bytes 1654786 | tf_op jit(solution)/shard_map/jit(_pad)/pad | solution.py:473
  3.6 0.0 copy-start.1
  3.6 66.7 %decoder.1 = bf16[2,208,256]{2,1,0:T(8,128)(2,1)} custom-call(s32[128]{0:T(128)} %partners_ref.1, bf16[2,208,1024]{2,1,0:T(8,128)(2,1)} %pad.7.past_hbm, bf16[2,208,1024]{2,1,0:T(8,128)(2,1)} %pad.8.current_hbm, bf16[1024,256]{1,0:T(8,128)(2,1)} %query_hbm.1, bf16[1024,256]{1,0:T(8,128)(2,1)} %key_hbm.1, bf16[1024,256]{1,0:T(8,128)(2,1)} %value_hbm.1, ...), custom_call_target="tpu_custom_call" | custom-call | tf_op jit(solution)/shard_map/decoder/pallas_call | solution.py:436
  70.3 0.0 copy-done.1
  70.3 0.1 iota_compare_fusion
  70.4 1.0 %slice_select_fusion = bf16[2,196,256]{2,1,0:T(8,128)(2,1)S(1)} fusion(bf16[2,208,256]{2,1,0:T(8,128)(2,1)} %decoder.1, pred[2,196]{1,0:T(4,128)(4,1)S(1)} %iota_compare_fusion), kind=kLoop, calls=%fused_computation | loop fusion | flops 100352 | bytes 401800 | tf_op jit(solution)/shard_map/jit(_where)/select_n | solution.py:482
  71.4 0.8 %copy.13 = bf16[2,196,256]{2,0,1:T(2,128)(2,1)} copy(bf16[2,196,256]{2,1,0:T(8,128)(2,1)S(1)} %slice_select_fusion) | data formatting | bytes 401408 | tf_op jit(solution)/shard_map/jit(_where)/select_n | solution.py:482
Async XLA Ops:
  0.0 2.4 %copy-start = (bf16[2,196,1024]{2,0,1:T(2,128)(2,1)S(1)}, bf16[2,196,1024]{2,0,1:T(2,128)(2,1)}, u32[]{:S(2)}) copy-start(bf16[2,196,1024]{2,0,1:T(2,128)(2,1)} %param.10) | copy-start | bytes 2408452
  3.6 66.7 %copy-start.1 = (s32[2]{0:T(128)S(1)}, s32[2]{0:T(128)}, u32[]{:S(2)}) copy-start(s32[2]{0:T(128)} %param.12) | copy-start | bytes 28

commit v3 on v2

v3 whole, which is shorter than its diff:
```python
import functools

import jax
import jax.numpy as jnp
from jax import lax
from jax.experimental import pallas as pl
from jax.experimental.pallas import tpu as pltpu
from jax.sharding import PartitionSpec as P

HEAD_DIM = 64
TILE = 16
LANES = 128
BLOCK_ROWS = 4
PIECES = 4
VMEM_LIMIT = 56 * 1024 * 1024
MESH = pl.DeviceIdType.MESH
F32 = jnp.float32
BF16 = jnp.bfloat16


class Ring:
    def __init__(self, part, rank, after, before, send, recv, base):
        def copy(index, owner, half, peer):
            ref = part(owner, half)
            return pltpu.make_async_remote_copy(
                src_ref=ref,
                dst_ref=ref,
                send_sem=send.at[base + index],
                recv_sem=recv.at[base + index],
                device_id={"mp": peer},
                device_id_type=MESH,
            )

        self.up = (copy(0, rank, 0, after), copy(1, rank, 1, after), copy(2, before, 0, after))
        self.down = (copy(3, rank, 1, before), copy(4, rank, 0, before), copy(5, after, 1, before))

    def start(self, step):
        self.up[step].start()
        self.down[step].start()

    def forward(self):
        self.up[0].wait_recv()
        self.up[2].start()
        self.down[0].wait_recv()
        self.down[2].start()

    def arrive(self):
        for step in (1, 2):
            self.up[step].wait_recv()
            self.down[step].wait_recv()

    def settle(self):
        for copy in self.up + self.down:
            copy.wait_send()


def stretches(rows, count):
    step = rows // count // TILE * TILE
    return [(k * step, rows if k == count - 1 else (k + 1) * step) for k in range(count)]


def normalized(values):
    center = values - jnp.mean(values, axis=-1, keepdims=True)
    spread = jnp.mean(center * center, axis=-1, keepdims=True)
    return (center * lax.rsqrt(spread + 1e-06)).astype(BF16)


def normalize(source, target, first, last):
    for start in range(first, last, TILE):
        stop = min(start + TILE, last)
        target[start:stop, :] = normalized(source[start:stop, :].astype(F32))


def flatten_and_normalize(source, target, first, last, kept=None):
    slots, width = source.shape[1:]
    for start in range(first, last, TILE):
        stop = min(start + TILE, last)
        tile = source[start // slots : stop // slots].reshape(stop - start, width)
        if kept is not None:
            kept[start:stop, :] = tile
        target[start:stop, :] = normalized(tile.astype(F32))


def put(target, first, last, result):
    for piece in range(target.shape[0]):
        target[piece, first:last, :] = result[:, piece * LANES : (piece + 1) * LANES]


def take(source, at):
    return jnp.concatenate([source[piece, at, :] for piece in range(source.shape[0])], axis=1)


def gelu(values):
    return 0.5 * values * (1.0 + lax.erf(values * (0.5**0.5)))


def decoder_kernel(
    groups,
    shards,
    partners_ref,
    past_hbm,
    current_hbm,
    query_hbm,
    key_hbm,
    value_hbm,
    output_hbm,
    up_hbm,
    down_hbm,
    out_ref,
    past,
    current,
    query_weight,
    key_weight,
    value_weight,
    output_weight,
    up_weight,
    down_weight,
    spread,
    sorted_tiles,
    context,
    flat,
    normed,
    queries,
    keys,
    values,
    mixed,
    attended,
    hidden,
    partial,
    packed,
    summed,
    landed,
    load,
    exchange_sem,
    ring_send,
    ring_recv,
):
    frame, slots, width = past.shape
    rows = frame * slots
    share = width // shards
    block_rows = spread.shape[1]
    kinds = frame // block_rows
    pieces = stretches(rows, PIECES)
    me = lax.axis_index("pair")
    rank = lax.axis_index("mp")
    column = pl.multiple_of(rank * share, LANES)
    after = lax.rem(rank + 1, shards)
    before = lax.rem(rank + shards - 1, shards)
    across = lax.rem(rank + 2, shards)
    core = lax.rem(me, 2)
    twin = me + 1 - 2 * core

    def fetch(index, source, target):
        copy = pltpu.make_async_copy(source, target, load.at[index])
        copy.start()
        return copy

    get_past = fetch(0, past_hbm, past)
    get_output = fetch(
        1, output_hbm, output_weight.at[pl.ds(pl.multiple_of(rank * share, share), share), :]
    )
    get_current = fetch(2, current_hbm, current)
    get_query = fetch(3, query_hbm, query_weight)
    get_key = fetch(4, key_hbm, key_weight)
    get_value = fetch(5, value_hbm, value_weight)
    get_up = fetch(6, up_hbm, up_weight)
    get_down = fetch(7, down_hbm, down_weight)

    def keeper(kind):
        return (kind * groups) // kinds

    mine = (me * kinds + groups - 1) // groups
    keeps = jnp.logical_and(mine < kinds, keeper(mine) == me)

    def place(kind):
        return pl.ds(kind * block_rows, block_rows), slice(None), pl.ds(column, share)

    barrier = pltpu.get_barrier_semaphore()

    def greet(step, carry):
        peer = lax.rem(me + 1 + step, groups)
        pl.semaphore_signal(barrier, inc=1, device_id={"pair": peer}, device_id_type=MESH)
        return carry

    lax.fori_loop(0, groups - 1, greet, 0)
    for peer in (after, before):
        pl.semaphore_signal(barrier, inc=1, device_id={"mp": peer}, device_id_type=MESH)
    pl.semaphore_wait(barrier, groups + 1)

    get_past.wait()
    first = (me * kinds) // groups

    def spread_one(step, carry):
        kind = lax.rem(first + step, kinds)
        target = keeper(kind)

        @pl.when(target != me)
        def _():
            pltpu.make_async_remote_copy(
                src_ref=past.at[place(kind)],
                dst_ref=spread.at[me],
                send_sem=exchange_sem.at[0],
                recv_sem=exchange_sem.at[1],
                device_id={"pair": target},
                device_id_type=MESH,
            ).start()

        @pl.when(target == me)
        def _():
            spread[me] = past[place(kind)]

        return carry

    lax.fori_loop(0, kinds, spread_one, 0)

    half = share // 2
    quarter = half // 2

    def weight_rows(owner, piece):
        row = pl.multiple_of(owner * share + core * half + piece * quarter, quarter)
        return output_weight.at[pl.ds(row, quarter), :]

    weight_ring = Ring(weight_rows, rank, after, before, ring_send, ring_recv, 0)
    get_output.wait()
    weight_ring.start(0)
    weight_ring.start(1)

    get_current.wait()
    get_query.wait()
    flatten_and_normalize(current, normed, 0, rows, flat)
    put(queries, 0, rows, jnp.dot(normed[...], query_weight[...], preferred_element_type=F32))

    @pl.when(keeps)
    def _():
        arrived = spread.at[pl.ds(0, groups - 1)]
        pltpu.make_async_copy(arrived, arrived, exchange_sem.at[1]).wait()
        slot = lax.broadcasted_iota(jnp.int32, spread.shape[1:], 1)

        def sort_one(step, carry):
            tile = spread[partners_ref[step * slots] // slots]
            for other in range(1, slots):
                tile = jnp.where(
                    slot == other, spread[partners_ref[step * slots + other] // slots], tile
                )
            sorted_tiles[step] = tile
            return carry

        lax.fori_loop(0, groups, sort_one, 0)
        context[place(mine)] = sorted_tiles[me]

        def deliver(step, carry):
            target = lax.rem(me + 1 + step, groups)
            pltpu.make_async_remote_copy(
                src_ref=sorted_tiles.at[target],
                dst_ref=context.at[place(mine)],
                send_sem=exchange_sem.at[2],
                recv_sem=exchange_sem.at[3],
                device_id={"pair": target},
                device_id_type=MESH,
            ).start()
            return carry

        lax.fori_loop(0, groups - 1, deliver, 0)

    weight_ring.forward()

    @pl.when(keeps)
    def _():
        got = spread.at[pl.ds(0, kinds - 1)]
        pltpu.make_async_copy(got, got, exchange_sem.at[3]).wait()

    @pl.when(jnp.logical_not(keeps))
    def _():
        got = spread.at[pl.ds(0, kinds)]
        pltpu.make_async_copy(got, got, exchange_sem.at[3]).wait()

    def lanes_of(owner, piece):
        return pl.ds(pl.multiple_of(owner * share + piece * LANES, LANES), LANES)

    def context_part(first, last):
        def part(owner, piece):
            return context.at[
                first // slots : last // slots, :, lanes_of(owner, piece)
            ]

        return part

    def attended_part(first, last):
        def part(owner, piece):
            return attended.at[first:last, lanes_of(owner, piece)]

        return part

    def rings(part, base):
        return [
            Ring(part(*piece), rank, after, before, ring_send, ring_recv, base + 6 * k)
            for k, piece in enumerate(pieces)
        ]

    context_rings = rings(context_part, 9)
    attended_rings = rings(attended_part, 9 + 6 * PIECES)
    for ring in context_rings:
        ring.start(0)
    for ring in context_rings[: PIECES // 2]:
        ring.start(1)
    weight_ring.arrive()

    def to_twin(index, owner):
        row = pl.multiple_of(owner * share + core * half, half)
        ref = output_weight.at[pl.ds(row, half), :]
        return pltpu.make_async_remote_copy(
            src_ref=ref,
            dst_ref=ref,
            send_sem=ring_send.at[6 + index],
            recv_sem=ring_recv.at[6 + index],
            device_id={"pair": twin},
            device_id_type=MESH,
        )

    twins = [to_twin(index, owner) for index, owner in enumerate((before, after, across))]
    for copy in twins:
        copy.start()
    for ring in context_rings[: PIECES // 2]:
        ring.forward()
    for ring in context_rings[PIECES // 2 :]:
        ring.start(1)
    for ring in context_rings[PIECES // 2 :]:
        ring.forward()

    get_key.wait()
    get_value.wait()
    for ring, (start, stop) in zip(context_rings, pieces):
        ring.arrive()
        flatten_and_normalize(context, normed, start, stop)
        for weight, target in ((key_weight, keys), (value_weight, values)):
            put(
                target,
                start,
                stop,
                jnp.dot(normed[start:stop, :], weight[...], preferred_element_type=F32),
            )

    heads = share // HEAD_DIM
    at_slot = [pl.ds(slot, frame, stride=slots) for slot in range(slots)]
    frame_keys = [take(keys, at).astype(BF16) for at in at_slot]
    frame_values = [take(values, at).astype(BF16) for at in at_slot]

    def attend(start, stop):
        count = -(-(stop - start) // slots // 8) * 8
        head_of = lax.broadcasted_iota(jnp.int32, (count, share), 1) // HEAD_DIM
        for slot in range(slots):
            at = pl.ds(start + slot, count, stride=slots)
            query = take(queries, at)
            stacked = jnp.concatenate(
                [jnp.where(head_of == head, query, 0.0) for head in range(heads)], axis=0
            ).astype(BF16)
            scores = (
                lax.dot_general(
                    stacked,
                    frame_keys[slot],
                    (((1,), (1,)), ((), ())),
                    preferred_element_type=F32,
                )
                * HEAD_DIM ** (-0.5)
            )
            lifted = jnp.exp(scores - jnp.max(scores, axis=-1, keepdims=True))
            weights = (lifted * (1.0 / jnp.sum(lifted, axis=-1, keepdims=True))).astype(BF16)
            spans = jnp.dot(weights, frame_values[slot], preferred_element_type=F32)
            total = spans[:count]
            for head in range(1, heads):
                total = jnp.where(head_of == head, spans[head * count : (head + 1) * count], total)
            for piece in range(mixed.shape[0]):
                mixed[piece, at, :] = total[:, piece * LANES : (piece + 1) * LANES]
        attended[start:stop, pl.ds(column, share)] = take(mixed, pl.ds(start, stop - start)).astype(
            BF16
        )

    for ring, piece in zip(attended_rings, pieces):
        attend(*piece)
        ring.start(0)
        ring.start(1)

    def sends(index, first, last):
        base = 9 + 12 * PIECES + 6 * index

        def copy(offset, source, peer):
            return pltpu.make_async_remote_copy(
                src_ref=source,
                dst_ref=landed.at[offset, first:last, :],
                send_sem=ring_send.at[base + offset],
                recv_sem=ring_recv.at[base + offset],
                device_id={"mp": peer},
                device_id_type=MESH,
            )

        return [
            copy(0, packed.at[first:last, lanes_of(across, 0)], after),
            copy(1, packed.at[first:last, lanes_of(across, 1)], before),
            copy(2, packed.at[first:last, lanes_of(after, 1)], after),
            copy(3, packed.at[first:last, lanes_of(before, 0)], before),
            copy(4, summed.at[0, first:last, :], after),
            copy(5, summed.at[1, first:last, :], before),
        ]

    reductions = [sends(index, *piece) for index, piece in enumerate(pieces)]

    def mix(index):
        first, last = pieces[index]
        hidden[first:last, :] = flat[first:last, :].astype(F32) + jnp.dot(
            attended[first:last, :], output_weight[...], preferred_element_type=F32
        )
        normalize(hidden, normed, first, last)
        expanded = gelu(
            jnp.dot(normed[first:last, :], up_weight[...], preferred_element_type=F32)
        ).astype(BF16)
        result = jnp.dot(expanded, down_weight[...], preferred_element_type=F32)
        partial[first:last, :] = result
        packed[first:last, :] = result.astype(BF16)
        for copy in reductions[index][:4]:
            copy.start()

    def relay(index):
        first, last = pieces[index]
        for piece, owner in ((0, after), (1, before)):
            reductions[index][piece].wait_recv()
            summed[piece, first:last, :] = (
                partial[first:last, lanes_of(owner, piece)]
                + landed[piece, first:last, :].astype(F32)
            ).astype(BF16)
            reductions[index][4 + piece].start()

    def finish(index):
        first, last = pieces[index]
        for copy in reductions[index][2:]:
            copy.wait_recv()
        for piece, others in ((0, (4, 3)), (1, (2, 5))):
            result = partial[first:last, lanes_of(rank, piece)]
            for other in others:
                result = result + landed[other, first:last, :].astype(F32)
            result = (hidden[first:last, lanes_of(rank, piece)] + result).astype(BF16)
            out_ref[
                first // slots : last // slots, :, piece * LANES : (piece + 1) * LANES
            ] = result.reshape((last - first) // slots, slots, LANES)

    for ring in attended_rings:
        ring.forward()
    for copy in twins:
        copy.wait_recv()
    get_up.wait()
    get_down.wait()
    for index, ring in enumerate(attended_rings):
        ring.arrive()
        mix(index)
        if index:
            relay(index - 1)
    relay(PIECES - 1)
    for index in range(PIECES):
        finish(index)

    for ring in [weight_ring] + context_rings + attended_rings:
        ring.settle()
    for copy in twins + sum(reductions, []):
        copy.wait_send()

    @pl.when(keeps)
    def _():
        left = spread.at[pl.ds(0, kinds - 1)]
        pltpu.make_async_copy(left, left, exchange_sem.at[0]).wait()
        sent = spread.at[pl.ds(0, groups - 1)]
        pltpu.make_async_copy(sent, sent, exchange_sem.at[2]).wait()

    @pl.when(jnp.logical_not(keeps))
    def _():
        left = spread.at[pl.ds(0, kinds)]
        pltpu.make_async_copy(left, left, exchange_sem.at[0]).wait()


def body(
    current,
    past_tokens,
    counts,
    partners,
    query_weight,
    key_weight,
    value_weight,
    output_weight,
    up_weight,
    down_weight,
):
    slots, frame, width = current.shape
    groups, shards = lax.axis_size("pair"), lax.axis_size("mp")
    share = width // shards
    features = query_weight.shape[1]
    hidden_units = up_weight.shape[1]
    rows = slots * frame
    spare = rows + TILE
    whole = pl.BlockSpec(memory_space=pltpu.HBM)
    packed_shape = (frame, slots, width)
    semaphores = 9 + 18 * PIECES
    result = pl.pallas_call(
        functools.partial(decoder_kernel, groups, shards),
        out_shape=jax.ShapeDtypeStruct((frame, slots, share), BF16),
        in_specs=[pl.BlockSpec(memory_space=pltpu.SMEM)] + [whole] * 8,
        out_specs=pl.BlockSpec(memory_space=pltpu.VMEM),
        scratch_shapes=[
            pltpu.VMEM(packed_shape, BF16),
            pltpu.VMEM(packed_shape, BF16),
            pltpu.VMEM((width, features), BF16),
            pltpu.VMEM((width, features), BF16),
            pltpu.VMEM((width, features), BF16),
            pltpu.VMEM((width, width), BF16),
            pltpu.VMEM((width, hidden_units), BF16),
            pltpu.VMEM((hidden_units, width), BF16),
            pltpu.VMEM((groups, BLOCK_ROWS, slots, share), BF16),
            pltpu.VMEM((groups, BLOCK_ROWS, slots, share), BF16),
            pltpu.VMEM(packed_shape, BF16),
            pltpu.VMEM((rows, width), BF16),
            pltpu.VMEM((rows, width), BF16),
            pltpu.VMEM((features // LANES, spare, LANES), F32),
            pltpu.VMEM((features // LANES, spare, LANES), F32),
            pltpu.VMEM((features // LANES, spare, LANES), F32),
            pltpu.VMEM((features // LANES, spare, LANES), F32),
            pltpu.VMEM((rows, width), BF16),
            pltpu.VMEM((rows, width), F32),
            pltpu.VMEM((rows, width), F32),
            pltpu.VMEM((rows, width), BF16),
            pltpu.VMEM((2, rows, LANES), BF16),
            pltpu.VMEM((6, rows, LANES), BF16),
            pltpu.SemaphoreType.DMA((8,)),
            pltpu.SemaphoreType.DMA((4,)),
            pltpu.SemaphoreType.DMA((semaphores,)),
            pltpu.SemaphoreType.DMA((semaphores,)),
        ],
        compiler_params=pltpu.CompilerParams(
            collective_id=0, has_side_effects=True, vmem_limit_bytes=VMEM_LIMIT
        ),
        name="decoder",
    )(
        partners,
        past_tokens.transpose(1, 0, 2),
        current.transpose(1, 0, 2),
        query_weight,
        key_weight,
        value_weight,
        output_weight,
        up_weight,
        down_weight,
    ).transpose(1, 0, 2)
    live = jnp.arange(frame, dtype=jnp.int32)[None, :, None] < counts[:, None, None]
    return jnp.where(live, result, jnp.zeros((), BF16))


def solution(mesh):
    placed = (
        P("pair", None, None),
        P("pair", None, None),
        P("pair"),
        P(),
        P(None, "mp"),
        P(None, "mp"),
        P(None, "mp"),
        P("mp", None),
        P(None, "mp"),
        P("mp", None),
    )
    return jax.shard_map(
        body, mesh=mesh, in_specs=placed, out_specs=P("pair", None, "mp"), check_vma=False
    )
```

time: 72.4 us -> 67.6 us (0.934)
  the two profiles are of different devices: /device:TPU:8 before, /device:TPU:32 now
where the time goes in v3:
time: 67.6 us; the launch traced here: 66.4 us
  Pallas kernels  63.8 us (94%)
  other arithmetic  2.61 us (4%)
    pallas_call x1, Pallas kernels, body(): pl.pallas_call(functools.partial(decoder_kernel, groups, shards), out_sha...  63.8 us
    select_n x1, other arithmetic, body(): return jnp.where(live, result, jnp.zeros((), BF16))  1.93 us

profile of v3, /device:TPU:32, one launch (start us, length us, event | category | flops | bytes accessed | tf_op | source)
XLA Modules:
  0.0 66.4 jit_solution(9620572561285010665)
XLA Ops:
  0.0 0.7 %iota_compare_fusion = pred[2,196]{0,1:T(8,128)(4,1)S(1)} fusion(s32[2]{0:T(128)} %param.12), kind=kLoop, calls=%fused_computation.1 | loop fusion | flops 392 | bytes 400 | tf_op jit(solution)/shard_map/lt | solution.py:549
  0.7 63.8 %decoder.1 = bf16[196,2,256]{2,1,0:T(2,128)(2,1)} custom-call(s32[128]{0:T(128)} %partners_ref.1, bf16[196,2,1024]{2,1,0:T(2,128)(2,1)} %bitcast.4, bf16[196,2,1024]{2,1,0:T(2,128)(2,1)} %bitcast.5, bf16[1024,256]{1,0:T(8,128)(2,1)} %query_hbm.1, bf16[1024,256]{1,0:T(8,128)(2,1)} %key_hbm.1, bf16[1024,256]{1,0:T(8,128)(2,1)} %value_hbm.1, ...), custom_call_target="tpu_custom_call" | custom-call | tf_op jit(solution)/shard_map/decoder/pallas_call | solution.py:500
  64.5 1.9 %broadcast_select_fusion = bf16[2,196,256]{2,0,1:T(2,128)(2,1)} fusion(pred[2,196]{0,1:T(8,128)(4,1)S(1)} %iota_compare_fusion, bf16[196,2,256]{2,1,0:T(2,128)(2,1)} %decoder.1), kind=kLoop, calls=%fused_computation | loop fusion | flops 100352 | bytes 401800 | tf_op jit(solution)/shard_map/jit(_where)/select_n | solution.py:550

commit v4 on v3

--- a/solution.py
+++ b/solution.py
@@ -1,4 +1,5 @@
 import functools
+import math
 
 import jax
 import jax.numpy as jnp
@@ -10,7 +11,7 @@
 HEAD_DIM = 64
 TILE = 16
 LANES = 128
-BLOCK_ROWS = 4
+BLOCK_ROWS = 7
 PIECES = 4
 VMEM_LIMIT = 56 * 1024 * 1024
 MESH = pl.DeviceIdType.MESH
@@ -98,6 +99,7 @@
     groups,
     shards,
     partners_ref,
+    counts_ref,
     past_hbm,
     current_hbm,
     query_hbm,
@@ -130,7 +132,9 @@
     packed,
     summed,
     landed,
+    out,
     load,
+    store,
     exchange_sem,
     ring_send,
     ring_recv,
@@ -139,7 +143,10 @@
     rows = frame * slots
     share = width // shards
     block_rows = spread.shape[1]
-    kinds = frame // block_rows
+    halves = share // LANES
+    kinds = frame // block_rows * halves
+    side = math.isqrt(groups)
+    keepers = kinds // side
     pieces = stretches(rows, PIECES)
     me = lax.axis_index("pair")
     rank = lax.axis_index("mp")
@@ -166,52 +173,65 @@
     get_up = fetch(6, up_hbm, up_weight)
     get_down = fetch(7, down_hbm, down_weight)
 
-    def keeper(kind):
-        return (kind * groups) // kinds
-
-    mine = (me * kinds + groups - 1) // groups
-    keeps = jnp.logical_and(mine < kinds, keeper(mine) == me)
+    square = me // side
+    seat = lax.rem(me, side)
+    keeps = seat < keepers
 
     def place(kind):
-        return pl.ds(kind * block_rows, block_rows), slice(None), pl.ds(column, share)
+        lane = pl.multiple_of(column + lax.rem(kind, halves) * LANES, LANES)
+        return pl.ds(kind // halves * block_rows, block_rows), slice(None), pl.ds(lane, LANES)
+
+    def other_square(step):
+        offset = (step + 1) // 2 * (1 - 2 * lax.rem(step, 2))
+        return lax.rem(square + side // 2 + offset, side)
+
+    def everyone(send):
+        def one_square(step, carry):
+            there = other_square(step)
+            for other in range(side):
+                send(there * side + other)
+            return carry
+
+        lax.fori_loop(0, side - 1, one_square, 0)
+        for other in range(1, side):
+            send(square * side + lax.rem(seat + other, side))
 
     barrier = pltpu.get_barrier_semaphore()
 
-    def greet(step, carry):
-        peer = lax.rem(me + 1 + step, groups)
+    def greet(peer):
         pl.semaphore_signal(barrier, inc=1, device_id={"pair": peer}, device_id_type=MESH)
-        return carry
-
-    lax.fori_loop(0, groups - 1, greet, 0)
+
+    everyone(greet)
     for peer in (after, before):
         pl.semaphore_signal(barrier, inc=1, device_id={"mp": peer}, device_id_type=MESH)
     pl.semaphore_wait(barrier, groups + 1)
 
     get_past.wait()
-    first = (me * kinds) // groups
-
-    def spread_one(step, carry):
-        kind = lax.rem(first + step, kinds)
-        target = keeper(kind)
-
-        @pl.when(target != me)
-        def _():
-            pltpu.make_async_remote_copy(
-                src_ref=past.at[place(kind)],
-                dst_ref=spread.at[me],
-                send_sem=exchange_sem.at[0],
-                recv_sem=exchange_sem.at[1],
-                device_id={"pair": target},
-                device_id_type=MESH,
-            ).start()
-
-        @pl.when(target == me)
-        def _():
-            spread[me] = past[place(kind)]
-
+
+    def spread_one(there, other):
+        pltpu.make_async_remote_copy(
+            src_ref=past.at[place(there * keepers + other)],
+            dst_ref=spread.at[me],
+            send_sem=exchange_sem.at[0],
+            recv_sem=exchange_sem.at[1],
+            device_id={"pair": there * side + other},
+            device_id_type=MESH,
+        ).start()
+
+    def spread_square(step, carry):
+        there = other_square(step)
+        for other in range(keepers):
+            spread_one(there, other)
         return carry
 
-    lax.fori_loop(0, kinds, spread_one, 0)
+    lax.fori_loop(0, side - 1, spread_square, 0)
+    mine = square * keepers + seat
+    for other in range(keepers):
+        pl.when(seat != other)(functools.partial(spread_one, square, other))
+
+    @pl.when(keeps)
+    def _():
+        spread[me] = past[place(mine)]
 
     half = share // 2
     quarter = half // 2
@@ -245,11 +265,10 @@
             sorted_tiles[step] = tile
             return carry
 
-        lax.fori_loop(0, groups, sort_one, 0)
+        lax.fori_loop(0, groups, sort_one, 0, unroll=8)
         context[place(mine)] = sorted_tiles[me]
 
-        def deliver(step, carry):
-            target = lax.rem(me + 1 + step, groups)
+        def deliver(target):
             pltpu.make_async_remote_copy(
                 src_ref=sorted_tiles.at[target],
                 dst_ref=context.at[place(mine)],
@@ -258,9 +277,8 @@
                 device_id={"pair": target},
                 device_id_type=MESH,
             ).start()
-            return carry
-
-        lax.fori_loop(0, groups - 1, deliver, 0)
+
+        everyone(deliver)
 
     weight_ring.forward()
 
@@ -375,10 +393,14 @@
             BF16
         )
 
-    for ring, piece in zip(attended_rings, pieces):
-        attend(*piece)
+    def launch(ring):
         ring.start(0)
         ring.start(1)
+
+    for index, piece in enumerate(pieces):
+        attend(*piece)
+        if index < 2:
+            launch(attended_rings[index])
 
     def sends(index, first, last):
         base = 9 + 12 * PIECES + 6 * index
@@ -437,13 +459,23 @@
             result = partial[first:last, lanes_of(rank, piece)]
             for other in others:
                 result = result + landed[other, first:last, :].astype(F32)
-            result = (hidden[first:last, lanes_of(rank, piece)] + result).astype(BF16)
-            out_ref[
+            row = first + lax.broadcasted_iota(jnp.int32, result.shape, 0)
+            limit = counts_ref[0]
+            for slot in range(1, slots):
+                limit = jnp.where(lax.rem(row, slots) == slot, counts_ref[slot], limit)
+            result = hidden[first:last, lanes_of(rank, piece)] + result
+            result = jnp.where(row // slots < limit, result, 0.0).astype(BF16)
+            out[
                 first // slots : last // slots, :, piece * LANES : (piece + 1) * LANES
             ] = result.reshape((last - first) // slots, slots, LANES)
-
-    for ring in attended_rings:
-        ring.forward()
+        at = slice(first // slots, last // slots)
+        pltpu.make_async_copy(out.at[at], out_ref.at[at], store.at[index]).start()
+
+    attended_rings[0].forward()
+    launch(attended_rings[2])
+    attended_rings[1].forward()
+    launch(attended_rings[3])
+    attended_rings[2].forward()
     for copy in twins:
         copy.wait_recv()
     get_up.wait()
@@ -451,12 +483,18 @@
     for index, ring in enumerate(attended_rings):
         ring.arrive()
         mix(index)
-        if index:
+        if index == 0:
+            attended_rings[3].forward()
+        else:
             relay(index - 1)
+    finish(0)
     relay(PIECES - 1)
-    for index in range(PIECES):
+    for index in range(1, PIECES):
         finish(index)
 
+    for index, (first, last) in enumerate(pieces):
+        at = slice(first // slots, last // slots)
+        pltpu.make_async_copy(out.at[at], out_ref.at[at], store.at[index]).wait()
     for ring in [weight_ring] + context_rings + attended_rings:
         ring.settle()
     for copy in twins + sum(reductions, []):
@@ -497,11 +535,11 @@
     whole = pl.BlockSpec(memory_space=pltpu.HBM)
     packed_shape = (frame, slots, width)
     semaphores = 9 + 18 * PIECES
-    result = pl.pallas_call(
+    return pl.pallas_call(
         functools.partial(decoder_kernel, groups, shards),
         out_shape=jax.ShapeDtypeStruct((frame, slots, share), BF16),
-        in_specs=[pl.BlockSpec(memory_space=pltpu.SMEM)] + [whole] * 8,
-        out_specs=pl.BlockSpec(memory_space=pltpu.VMEM),
+        in_specs=[pl.BlockSpec(memory_space=pltpu.SMEM)] * 2 + [whole] * 8,
+        out_specs=whole,
         scratch_shapes=[
             pltpu.VMEM(packed_shape, BF16),
             pltpu.VMEM(packed_shape, BF16),
@@ -511,8 +549,8 @@
             pltpu.VMEM((width, width), BF16),
             pltpu.VMEM((width, hidden_units), BF16),
             pltpu.VMEM((hidden_units, width), BF16),
-            pltpu.VMEM((groups, BLOCK_ROWS, slots, share), BF16),
-            pltpu.VMEM((groups, BLOCK_ROWS, slots, share), BF16),
+            pltpu.VMEM((groups, BLOCK_ROWS, slots, LANES), BF16),
+            pltpu.VMEM((groups, BLOCK_ROWS, slots, LANES), BF16),
             pltpu.VMEM(packed_shape, BF16),
             pltpu.VMEM((rows, width), BF16),
             pltpu.VMEM((rows, width), BF16),
@@ -526,7 +564,9 @@
             pltpu.VMEM((rows, width), BF16),
             pltpu.VMEM((2, rows, LANES), BF16),
             pltpu.VMEM((6, rows, LANES), BF16),
+            pltpu.VMEM((frame, slots, share), BF16),
             pltpu.SemaphoreType.DMA((8,)),
+            pltpu.SemaphoreType.DMA((PIECES,)),
             pltpu.SemaphoreType.DMA((4,)),
             pltpu.SemaphoreType.DMA((semaphores,)),
             pltpu.SemaphoreType.DMA((semaphores,)),
@@ -537,6 +577,7 @@
         name="decoder",
     )(
         partners,
+        counts,
         past_tokens.transpose(1, 0, 2),
         current.transpose(1, 0, 2),
         query_weight,
@@ -546,8 +587,6 @@
         up_weight,
         down_weight,
     ).transpose(1, 0, 2)
-    live = jnp.arange(frame, dtype=jnp.int32)[None, :, None] < counts[:, None, None]
-    return jnp.where(live, result, jnp.zeros((), BF16))
 
 
 def solution(mesh):

time: 67.6 us -> 64.4 us (0.953)
  the two profiles are of different devices: /device:TPU:32 before, /device:TPU:8 now
where the time goes in v4:
time: 64.4 us; the launch traced here: 64.3 us
  Pallas kernels  62.5 us (97%)
  local copies, waits for them, and re-layouts  1.75 us (3%)
    pallas_call x1, Pallas kernels, body(): pl.pallas_call(functools.partial(decoder_kernel, groups, shards), out_sha...  62.5 us
    unnamed x1, local copies, waits for them, and re-layouts  1.75 us

profile of v4, /device:TPU:8, one launch (start us, length us, event | category | flops | bytes accessed | tf_op | source)
XLA Modules:
  0.0 64.3 jit_solution(17730233206873616533)
XLA Ops:
  0.0 62.5 %decoder.1 = bf16[196,2,256]{2,1,0:T(2,128)(2,1)} custom-call(s32[128]{0:T(128)} %partners_ref.1, s32[2]{0:T(128)} %counts_ref.1, bf16[196,2,1024]{2,1,0:T(2,128)(2,1)} %bitcast.4, bf16[196,2,1024]{2,1,0:T(2,128)(2,1)} %bitcast.5, bf16[1024,256]{1,0:T(8,128)(2,1)} %query_hbm.1, bf16[1024,256]{1,0:T(8,128)(2,1)} %key_hbm.1, bf16[1024,256]{1,0:T(8,128)(2,1)} %value_hbm.1, ...), custom_call_target="tpu_custom_call" | custom-call | tf_op jit(solution)/shard_map/decoder/pallas_call | solution.py:538
  62.5 1.7 %copy.12 = bf16[2,196,256]{2,0,1:T(2,128)(2,1)} copy(bf16[2,196,256]{2,0,1:T(2,128)(2,1)} %bitcast.3) | data formatting | bytes 401408

commit v5 on v4

--- a/solution.py
+++ b/solution.py
@@ -185,6 +185,23 @@
         offset = (step + 1) // 2 * (1 - 2 * lax.rem(step, 2))
         return lax.rem(square + side // 2 + offset, side)
 
+    group = side // 2
+    part = square // group
+    corner = lax.rem(square, group)
+    frame_part = frame // 2
+
+    def own_half_first(send):
+        for step in (2, 1, 3):
+            there = part * group + lax.rem(corner + step, group)
+            for other in range(side):
+                send(there * side + other)
+        for other in range(1, side):
+            send(square * side + lax.rem(seat + other, side))
+        for step in (0, 1, 3, 2):
+            there = (1 - part) * group + lax.rem(corner + step, group)
+            for other in range(side):
+                send(there * side + other)
+
     def everyone(send):
         def one_square(step, carry):
             there = other_square(step)
@@ -248,7 +265,9 @@
     get_current.wait()
     get_query.wait()
     flatten_and_normalize(current, normed, 0, rows, flat)
-    put(queries, 0, rows, jnp.dot(normed[...], query_weight[...], preferred_element_type=F32))
+    put(
+        queries, 0, rows, jnp.dot(normed[0:rows, :], query_weight[...], preferred_element_type=F32)
+    )
 
     @pl.when(keeps)
     def _():
@@ -273,35 +292,36 @@
                 src_ref=sorted_tiles.at[target],
                 dst_ref=context.at[place(mine)],
                 send_sem=exchange_sem.at[2],
-                recv_sem=exchange_sem.at[3],
+                recv_sem=exchange_sem.at[3 + part],
                 device_id={"pair": target},
                 device_id_type=MESH,
             ).start()
 
-        everyone(deliver)
+        own_half_first(deliver)
 
     weight_ring.forward()
 
     @pl.when(keeps)
     def _():
-        got = spread.at[pl.ds(0, kinds - 1)]
-        pltpu.make_async_copy(got, got, exchange_sem.at[3]).wait()
+        got = spread.at[pl.ds(0, kinds // 2 - 1)]
+        pltpu.make_async_copy(got, got, exchange_sem.at[3 + part]).wait()
 
     @pl.when(jnp.logical_not(keeps))
     def _():
-        got = spread.at[pl.ds(0, kinds)]
-        pltpu.make_async_copy(got, got, exchange_sem.at[3]).wait()
+        got = spread.at[pl.ds(0, kinds // 2)]
+        pltpu.make_async_copy(got, got, exchange_sem.at[3 + part]).wait()
 
     def lanes_of(owner, piece):
         return pl.ds(pl.multiple_of(owner * share + piece * LANES, LANES), LANES)
 
-    def context_part(first, last):
-        def part(owner, piece):
-            return context.at[
-                first // slots : last // slots, :, lanes_of(owner, piece)
-            ]
-
-        return part
+    def context_part(index):
+        size = frame_part // 2
+        start = (part if index < 2 else 1 - part) * frame_part + index % 2 * size
+
+        def of(owner, piece):
+            return context.at[pl.ds(start, size), :, lanes_of(owner, piece)]
+
+        return of
 
     def attended_part(first, last):
         def part(owner, piece):
@@ -309,17 +329,21 @@
 
         return part
 
-    def rings(part, base):
-        return [
-            Ring(part(*piece), rank, after, before, ring_send, ring_recv, base + 6 * k)
-            for k, piece in enumerate(pieces)
-        ]
-
-    context_rings = rings(context_part, 9)
-    attended_rings = rings(attended_part, 9 + 6 * PIECES)
-    for ring in context_rings:
+    def make_ring(of, base):
+        return Ring(of, rank, after, before, ring_send, ring_recv, base)
+
+    context_rings = [make_ring(context_part(k), 9 + 6 * k) for k in range(4)]
+    attended_rings = [
+        make_ring(attended_part(*piece), 33 + 6 * k) for k, piece in enumerate(pieces)
+    ]
+
+    def launch(ring):
         ring.start(0)
-    for ring in context_rings[: PIECES // 2]:
+        ring.start(1)
+
+    for ring in context_rings[:2]:
+        ring.start(0)
+    for ring in context_rings[:2]:
         ring.start(1)
     weight_ring.arrive()
 
@@ -338,30 +362,51 @@
     twins = [to_twin(index, owner) for index, owner in enumerate((before, after, across))]
     for copy in twins:
         copy.start()
-    for ring in context_rings[: PIECES // 2]:
+    for ring in context_rings[:2]:
         ring.forward()
-    for ring in context_rings[PIECES // 2 :]:
+    got = spread.at[pl.ds(0, kinds // 2)]
+    pltpu.make_async_copy(got, got, exchange_sem.at[3 + 1 - part]).wait()
+    for ring in context_rings[2:]:
+        ring.start(0)
+    for ring in context_rings[2:]:
         ring.start(1)
-    for ring in context_rings[PIECES // 2 :]:
-        ring.forward()
 
     get_key.wait()
     get_value.wait()
-    for ring, (start, stop) in zip(context_rings, pieces):
-        ring.arrive()
-        flatten_and_normalize(context, normed, start, stop)
+    part_rows = frame_part * slots
+
+    def project(index):
+        at = part if index == 0 else 1 - part
+        base = index * (normed.shape[0] // 2)
+        for start in range(0, part_rows, TILE):
+            count = min(TILE, part_rows - start)
+            tile = context[pl.ds(at * frame_part + start // slots, count // slots)]
+            normed[base + start : base + start + count, :] = normalized(
+                tile.reshape(count, width).astype(F32)
+            )
         for weight, target in ((key_weight, keys), (value_weight, values)):
-            put(
-                target,
-                start,
-                stop,
-                jnp.dot(normed[start:stop, :], weight[...], preferred_element_type=F32),
+            result = jnp.dot(
+                normed[base : base + part_rows, :], weight[...], preferred_element_type=F32
             )
+            for piece in range(halves):
+                target[at, piece, 0:part_rows, :] = result[:, piece * LANES : (piece + 1) * LANES]
+
+    for index in range(2):
+        for ring in context_rings[2 * index : 2 * index + 2]:
+            if index:
+                ring.forward()
+        for ring in context_rings[2 * index : 2 * index + 2]:
+            ring.arrive()
+        project(index)
 
     heads = share // HEAD_DIM
-    at_slot = [pl.ds(slot, frame, stride=slots) for slot in range(slots)]
-    frame_keys = [take(keys, at).astype(BF16) for at in at_slot]
-    frame_values = [take(values, at).astype(BF16) for at in at_slot]
+
+    def of_slot(source, slot):
+        at = pl.ds(slot, frame_part, stride=slots)
+        return jnp.concatenate([take(source.at[k], at) for k in range(2)], axis=0).astype(BF16)
+
+    frame_keys = [of_slot(keys, slot) for slot in range(slots)]
+    frame_values = [of_slot(values, slot) for slot in range(slots)]
 
     def attend(start, stop):
         count = -(-(stop - start) // slots // 8) * 8
@@ -393,17 +438,13 @@
             BF16
         )
 
-    def launch(ring):
-        ring.start(0)
-        ring.start(1)
-
     for index, piece in enumerate(pieces):
         attend(*piece)
         if index < 2:
             launch(attended_rings[index])
 
     def sends(index, first, last):
-        base = 9 + 12 * PIECES + 6 * index
+        base = 33 + 6 * PIECES + 6 * index
 
         def copy(offset, source, peer):
             return pltpu.make_async_remote_copy(
@@ -532,9 +573,10 @@
     hidden_units = up_weight.shape[1]
     rows = slots * frame
     spare = rows + TILE
+    half_rows = -(-rows // 2 // TILE) * TILE
     whole = pl.BlockSpec(memory_space=pltpu.HBM)
     packed_shape = (frame, slots, width)
-    semaphores = 9 + 18 * PIECES
+    semaphores = 33 + 12 * PIECES
     return pl.pallas_call(
         functools.partial(decoder_kernel, groups, shards),
         out_shape=jax.ShapeDtypeStruct((frame, slots, share), BF16),
@@ -553,10 +595,10 @@
             pltpu.VMEM((groups, BLOCK_ROWS, slots, LANES), BF16),
             pltpu.VMEM(packed_shape, BF16),
             pltpu.VMEM((rows, width), BF16),
-            pltpu.VMEM((rows, width), BF16),
+            pltpu.VMEM((2 * half_rows, width), BF16),
             pltpu.VMEM((features // LANES, spare, LANES), F32),
-            pltpu.VMEM((features // LANES, spare, LANES), F32),
-            pltpu.VMEM((features // LANES, spare, LANES), F32),
+            pltpu.VMEM((2, features // LANES, half_rows, LANES), F32),
+            pltpu.VMEM((2, features // LANES, half_rows, LANES), F32),
             pltpu.VMEM((features // LANES, spare, LANES), F32),
             pltpu.VMEM((rows, width), BF16),
             pltpu.VMEM((rows, width), F32),
@@ -567,7 +609,7 @@
             pltpu.VMEM((frame, slots, share), BF16),
             pltpu.SemaphoreType.DMA((8,)),
             pltpu.SemaphoreType.DMA((PIECES,)),
-            pltpu.SemaphoreType.DMA((4,)),
+            pltpu.SemaphoreType.DMA((5,)),
             pltpu.SemaphoreType.DMA((semaphores,)),
             pltpu.SemaphoreType.DMA((semaphores,)),
         ],

time: 64.4 us -> 64.5 us (level)
  the two profiles are of different devices: /device:TPU:8 before, /device:TPU:32 now
where the time goes in v5:
time: 64.5 us; the launch traced here: 64.3 us
  Pallas kernels  62.5 us (97%)
  local copies, waits for them, and re-layouts  1.75 us (3%)
    pallas_call x1, Pallas kernels, body(): pl.pallas_call(functools.partial(decoder_kernel, groups, shards), out_sha...  62.5 us
    unnamed x1, local copies, waits for them, and re-layouts  1.75 us

profile of v5, /device:TPU:32, one launch (start us, length us, event | category | flops | bytes accessed | tf_op | source)
XLA Modules:
  0.0 64.3 jit_solution(17900605642644004122)
XLA Ops:
  0.0 62.5 %decoder.1 = bf16[196,2,256]{2,1,0:T(2,128)(2,1)} custom-call(s32[128]{0:T(128)} %partners_ref.1, s32[2]{0:T(128)} %counts_ref.1, bf16[196,2,1024]{2,1,0:T(2,128)(2,1)} %bitcast.4, bf16[196,2,1024]{2,1,0:T(2,128)(2,1)} %bitcast.5, bf16[1024,256]{1,0:T(8,128)(2,1)} %query_hbm.1, bf16[1024,256]{1,0:T(8,128)(2,1)} %key_hbm.1, bf16[1024,256]{1,0:T(8,128)(2,1)} %value_hbm.1, ...), custom_call_target="tpu_custom_call" | custom-call | tf_op jit(solution)/shard_map/decoder/pallas_call | solution.py:580
  62.5 1.7 %copy.12 = bf16[2,196,256]{2,0,1:T(2,128)(2,1)} copy(bf16[2,196,256]{2,0,1:T(2,128)(2,1)} %bitcast.3) | data formatting | bytes 401408

commit v6 on v5

--- a/solution.py
+++ b/solution.py
@@ -12,7 +12,7 @@
 TILE = 16
 LANES = 128
 BLOCK_ROWS = 7
-PIECES = 4
+CUTS = (96, 240)
 VMEM_LIMIT = 56 * 1024 * 1024
 MESH = pl.DeviceIdType.MESH
 F32 = jnp.float32
@@ -53,11 +53,6 @@
     def settle(self):
         for copy in self.up + self.down:
             copy.wait_send()
-
-
-def stretches(rows, count):
-    step = rows // count // TILE * TILE
-    return [(k * step, rows if k == count - 1 else (k + 1) * step) for k in range(count)]
 
 
 def normalized(values):
@@ -147,7 +142,8 @@
     kinds = frame // block_rows * halves
     side = math.isqrt(groups)
     keepers = kinds // side
-    pieces = stretches(rows, PIECES)
+    pieces = list(zip((0,) + CUTS, CUTS + (rows,)))
+    last_piece = len(pieces) - 1
     me = lax.axis_index("pair")
     rank = lax.axis_index("mp")
     column = pl.multiple_of(rank * share, LANES)
@@ -190,17 +186,12 @@
     corner = lax.rem(square, group)
     frame_part = frame // 2
 
-    def own_half_first(send):
-        for step in (2, 1, 3):
-            there = part * group + lax.rem(corner + step, group)
-            for other in range(side):
-                send(there * side + other)
-        for other in range(1, side):
-            send(square * side + lax.rem(seat + other, side))
-        for step in (0, 1, 3, 2):
-            there = (1 - part) * group + lax.rem(corner + step, group)
-            for other in range(side):
-                send(there * side + other)
+    def delivery_squares():
+        near = [part * group + lax.rem(corner + step, group) for step in (2, 1, 3)]
+        far = [(1 - part) * group + lax.rem(corner + step, group) for step in (0, 1, 3, 2)]
+        own = [square * side + lax.rem(seat + other, side) for other in range(1, side)]
+        whole = [[there * side + other for other in range(side)] for there in near + far]
+        return whole[:3] + [own] + whole[3:]
 
     def everyone(send):
         def one_square(step, carry):
@@ -269,23 +260,21 @@
         queries, 0, rows, jnp.dot(normed[0:rows, :], query_weight[...], preferred_element_type=F32)
     )
 
+    weight_ring.forward()
+
     @pl.when(keeps)
     def _():
         arrived = spread.at[pl.ds(0, groups - 1)]
         pltpu.make_async_copy(arrived, arrived, exchange_sem.at[1]).wait()
         slot = lax.broadcasted_iota(jnp.int32, spread.shape[1:], 1)
 
-        def sort_one(step, carry):
+        def sort_one(step):
             tile = spread[partners_ref[step * slots] // slots]
             for other in range(1, slots):
                 tile = jnp.where(
                     slot == other, spread[partners_ref[step * slots + other] // slots], tile
                 )
             sorted_tiles[step] = tile
-            return carry
-
-        lax.fori_loop(0, groups, sort_one, 0, unroll=8)
-        context[place(mine)] = sorted_tiles[me]
 
         def deliver(target):
             pltpu.make_async_remote_copy(
@@ -297,9 +286,17 @@
                 device_id_type=MESH,
             ).start()
 
-        own_half_first(deliver)
-
-    weight_ring.forward()
+        waiting = []
+        for targets in delivery_squares():
+            for target in targets:
+                sort_one(target)
+            for target in waiting:
+                deliver(target)
+            waiting = targets
+        sort_one(me)
+        context[place(mine)] = sorted_tiles[me]
+        for target in waiting:
+            deliver(target)
 
     @pl.when(keeps)
     def _():
@@ -391,10 +388,9 @@
             for piece in range(halves):
                 target[at, piece, 0:part_rows, :] = result[:, piece * LANES : (piece + 1) * LANES]
 
+    for ring in context_rings[2:]:
+        ring.forward()
     for index in range(2):
-        for ring in context_rings[2 * index : 2 * index + 2]:
-            if index:
-                ring.forward()
         for ring in context_rings[2 * index : 2 * index + 2]:
             ring.arrive()
         project(index)
@@ -444,7 +440,7 @@
             launch(attended_rings[index])
 
     def sends(index, first, last):
-        base = 33 + 6 * PIECES + 6 * index
+        base = 33 + 6 * len(pieces) + 6 * index
 
         def copy(offset, source, peer):
             return pltpu.make_async_remote_copy(
@@ -512,11 +508,10 @@
         at = slice(first // slots, last // slots)
         pltpu.make_async_copy(out.at[at], out_ref.at[at], store.at[index]).start()
 
-    attended_rings[0].forward()
-    launch(attended_rings[2])
-    attended_rings[1].forward()
-    launch(attended_rings[3])
-    attended_rings[2].forward()
+    for index in range(last_piece):
+        attended_rings[index].forward()
+        if index + 2 <= last_piece:
+            launch(attended_rings[index + 2])
     for copy in twins:
         copy.wait_recv()
     get_up.wait()
@@ -525,12 +520,13 @@
         ring.arrive()
         mix(index)
         if index == 0:
-            attended_rings[3].forward()
+            attended_rings[last_piece].forward()
         else:
             relay(index - 1)
-    finish(0)
-    relay(PIECES - 1)
-    for index in range(1, PIECES):
+    for index in range(last_piece - 1):
+        finish(index)
+    relay(last_piece)
+    for index in range(last_piece - 1, last_piece + 1):
         finish(index)
 
     for index, (first, last) in enumerate(pieces):
@@ -576,7 +572,7 @@
     half_rows = -(-rows // 2 // TILE) * TILE
     whole = pl.BlockSpec(memory_space=pltpu.HBM)
     packed_shape = (frame, slots, width)
-    semaphores = 33 + 12 * PIECES
+    semaphores = 33 + 12 * (len(CUTS) + 1)
     return pl.pallas_call(
         functools.partial(decoder_kernel, groups, shards),
         out_shape=jax.ShapeDtypeStruct((frame, slots, share), BF16),
@@ -608,7 +604,7 @@
             pltpu.VMEM((6, rows, LANES), BF16),
             pltpu.VMEM((frame, slots, share), BF16),
             pltpu.SemaphoreType.DMA((8,)),
-            pltpu.SemaphoreType.DMA((PIECES,)),
+            pltpu.SemaphoreType.DMA((len(CUTS) + 1,)),
             pltpu.SemaphoreType.DMA((5,)),
             pltpu.SemaphoreType.DMA((semaphores,)),
             pltpu.SemaphoreType.DMA((semaphores,)),

time: 64.5 us -> 63.3 us (0.981)
  Pallas kernels: 62.5 us -> 61.5 us
    pallas_call x1, Pallas kernels: 62.5 us -> 61.5 us  [body(): pl.pallas_call(functools.partial(decoder_kernel, groups, shards), out_sha...]
where the time goes in v6:
time: 63.3 us; the launch traced here: 63.2 us
  Pallas kernels  61.5 us (97%)
  local copies, waits for them, and re-layouts  1.75 us (3%)
    pallas_call x1, Pallas kernels, body(): pl.pallas_call(functools.partial(decoder_kernel, groups, shards), out_sha...  61.5 us
    unnamed x1, local copies, waits for them, and re-layouts  1.75 us

profile of v6, /device:TPU:32, one launch (start us, length us, event | category | flops | bytes accessed | tf_op | source)
XLA Modules:
  0.0 63.2 jit_solution(4162501539544486046)
XLA Ops:
  0.0 61.5 %decoder.1 = bf16[196,2,256]{2,1,0:T(2,128)(2,1)} custom-call(s32[128]{0:T(128)} %partners_ref.1, s32[2]{0:T(128)} %counts_ref.1, bf16[196,2,1024]{2,1,0:T(2,128)(2,1)} %bitcast.4, bf16[196,2,1024]{2,1,0:T(2,128)(2,1)} %bitcast.5, bf16[1024,256]{1,0:T(8,128)(2,1)} %query_hbm.1, bf16[1024,256]{1,0:T(8,128)(2,1)} %key_hbm.1, bf16[1024,256]{1,0:T(8,128)(2,1)} %value_hbm.1, ...), custom_call_target="tpu_custom_call" | custom-call | tf_op jit(solution)/shard_map/decoder/pallas_call | solution.py:576
  61.5 1.7 %copy.12 = bf16[2,196,256]{2,0,1:T(2,128)(2,1)} copy(bf16[2,196,256]{2,0,1:T(2,128)(2,1)} %bitcast.3) | data formatting | bytes 401408

commit v7 on v6

--- a/solution.py
+++ b/solution.py
@@ -12,8 +12,8 @@
 TILE = 16
 LANES = 128
 BLOCK_ROWS = 7
-CUTS = (96, 240)
-VMEM_LIMIT = 56 * 1024 * 1024
+CUTS = (112, 272)
+VMEM_LIMIT = 54784 * 1024
 MESH = pl.DeviceIdType.MESH
 F32 = jnp.float32
 BF16 = jnp.bfloat16
@@ -127,9 +127,7 @@
     packed,
     summed,
     landed,
-    out,
     load,
-    store,
     exchange_sem,
     ring_send,
     ring_recv,
@@ -502,11 +500,9 @@
                 limit = jnp.where(lax.rem(row, slots) == slot, counts_ref[slot], limit)
             result = hidden[first:last, lanes_of(rank, piece)] + result
             result = jnp.where(row // slots < limit, result, 0.0).astype(BF16)
-            out[
+            out_ref[
                 first // slots : last // slots, :, piece * LANES : (piece + 1) * LANES
             ] = result.reshape((last - first) // slots, slots, LANES)
-        at = slice(first // slots, last // slots)
-        pltpu.make_async_copy(out.at[at], out_ref.at[at], store.at[index]).start()
 
     for index in range(last_piece):
         attended_rings[index].forward()
@@ -529,9 +525,6 @@
     for index in range(last_piece - 1, last_piece + 1):
         finish(index)
 
-    for index, (first, last) in enumerate(pieces):
-        at = slice(first // slots, last // slots)
-        pltpu.make_async_copy(out.at[at], out_ref.at[at], store.at[index]).wait()
     for ring in [weight_ring] + context_rings + attended_rings:
         ring.settle()
     for copy in twins + sum(reductions, []):
@@ -577,7 +570,7 @@
         functools.partial(decoder_kernel, groups, shards),
         out_shape=jax.ShapeDtypeStruct((frame, slots, share), BF16),
         in_specs=[pl.BlockSpec(memory_space=pltpu.SMEM)] * 2 + [whole] * 8,
-        out_specs=whole,
+        out_specs=pl.BlockSpec(memory_space=pltpu.VMEM),
         scratch_shapes=[
             pltpu.VMEM(packed_shape, BF16),
             pltpu.VMEM(packed_shape, BF16),
@@ -602,9 +595,7 @@
             pltpu.VMEM((rows, width), BF16),
             pltpu.VMEM((2, rows, LANES), BF16),
             pltpu.VMEM((6, rows, LANES), BF16),
-            pltpu.VMEM((frame, slots, share), BF16),
             pltpu.SemaphoreType.DMA((8,)),
-            pltpu.SemaphoreType.DMA((len(CUTS) + 1,)),
             pltpu.SemaphoreType.DMA((5,)),
             pltpu.SemaphoreType.DMA((semaphores,)),
             pltpu.SemaphoreType.DMA((semaphores,)),

time: 63.3 us -> 62.4 us (0.986)
  Pallas kernels: 61.5 us -> 60.3 us
    pallas_call x1, Pallas kernels: 61.5 us -> 60.3 us  [body(): pl.pallas_call(functools.partial(decoder_kernel, groups, shards), out_sha...]
    unnamed x1 -> x5, local copies, waits for them, and re-layouts: 1.75 us -> 1.99 us
where the time goes in v7:
time: 62.4 us; the launch traced here: 62.3 us
  Pallas kernels  60.3 us (97%)
  local copies, waits for them, and re-layouts  1.99 us (3%)
    pallas_call x1, Pallas kernels, body(): pl.pallas_call(functools.partial(decoder_kernel, groups, shards), out_sha...  60.3 us
    unnamed x5, local copies, waits for them, and re-layouts  1.99 us

profile of v7, /device:TPU:32, one launch (start us, length us, event | category | flops | bytes accessed | tf_op | source)
XLA Modules:
  0.0 62.3 jit_solution(6057464471168388595)
XLA Ops:
  0.0 0.0 copy-start
  0.0 0.7 %copy-done = s32[128]{0:T(128)S(1)} copy-done((s32[128]{0:T(128)S(1)}, s32[128]{0:T(128)}, u32[]{:S(2)}) %copy-start) | copy-done | bytes 536
  0.7 0.0 copy-start.1
  0.7 0.7 %copy-done.1 = s32[2]{0:T(128)S(1)} copy-done((s32[2]{0:T(128)S(1)}, s32[2]{0:T(128)}, u32[]{:S(2)}) %copy-start.1) | copy-done | bytes 32
  1.3 60.3 %decoder.1 = bf16[196,2,256]{2,1,0:T(2,128)(2,1)S(1)} custom-call(s32[128]{0:T(128)S(1)} %copy-done, s32[2]{0:T(128)S(1)} %copy-done.1, bf16[196,2,1024]{2,1,0:T(2,128)(2,1)} %bitcast.4, bf16[196,2,1024]{2,1,0:T(2,128)(2,1)} %bitcast.5, bf16[1024,256]{1,0:T(8,128)(2,1)} %query_hbm.1, bf16[1024,256]{1,0:T(8,128)(2,1)} %key_hbm.1, ...), custom_call_target="tpu_custom_call" | custom-call | tf_op jit(solution)/shard_map/decoder/pallas_call | solution.py:569
  61.6 0.7 %copy.12 = bf16[2,196,256]{2,0,1:T(2,128)(2,1)} copy(bf16[2,196,256]{2,0,1:T(2,128)(2,1)S(1)} %bitcast.3) | data formatting | bytes 401408
Async XLA Ops:
  0.0 0.7 %copy-start = (s32[128]{0:T(128)S(1)}, s32[128]{0:T(128)}, u32[]{:S(2)}) copy-start(s32[128]{0:T(128)} %partners_ref.1) | copy-start | bytes 1540
  0.7 0.7 %copy-start.1 = (s32[2]{0:T(128)S(1)}, s32[2]{0:T(128)}, u32[]{:S(2)}) copy-start(s32[2]{0:T(128)} %counts_ref.1) | copy-start | bytes 28

commit v8 on v7

--- a/solution.py
+++ b/solution.py
@@ -93,8 +93,7 @@
 def decoder_kernel(
     groups,
     shards,
-    partners_ref,
-    counts_ref,
+    table_ref,
     past_hbm,
     current_hbm,
     query_hbm,
@@ -267,10 +266,10 @@
         slot = lax.broadcasted_iota(jnp.int32, spread.shape[1:], 1)
 
         def sort_one(step):
-            tile = spread[partners_ref[step * slots] // slots]
+            tile = spread[table_ref[step * slots] // slots]
             for other in range(1, slots):
                 tile = jnp.where(
-                    slot == other, spread[partners_ref[step * slots + other] // slots], tile
+                    slot == other, spread[table_ref[step * slots + other] // slots], tile
                 )
             sorted_tiles[step] = tile
 
@@ -495,9 +494,9 @@
             for other in others:
                 result = result + landed[other, first:last, :].astype(F32)
             row = first + lax.broadcasted_iota(jnp.int32, result.shape, 0)
-            limit = counts_ref[0]
+            limit = table_ref[groups * slots]
             for slot in range(1, slots):
-                limit = jnp.where(lax.rem(row, slots) == slot, counts_ref[slot], limit)
+                limit = jnp.where(lax.rem(row, slots) == slot, table_ref[groups * slots + slot], limit)
             result = hidden[first:last, lanes_of(rank, piece)] + result
             result = jnp.where(row // slots < limit, result, 0.0).astype(BF16)
             out_ref[
@@ -569,7 +568,7 @@
     return pl.pallas_call(
         functools.partial(decoder_kernel, groups, shards),
         out_shape=jax.ShapeDtypeStruct((frame, slots, share), BF16),
-        in_specs=[pl.BlockSpec(memory_space=pltpu.SMEM)] * 2 + [whole] * 8,
+        in_specs=[pl.BlockSpec(memory_space=pltpu.SMEM)] + [whole] * 8,
         out_specs=pl.BlockSpec(memory_space=pltpu.VMEM),
         scratch_shapes=[
             pltpu.VMEM(packed_shape, BF16),
@@ -605,8 +604,7 @@
         ),
         name="decoder",
     )(
-        partners,
-        counts,
+        jnp.concatenate([partners, counts]),
         past_tokens.transpose(1, 0, 2),
         current.transpose(1, 0, 2),
         query_weight,

time: 62.4 us -> 61.7 us (0.989)
  local copies, waits for them, and re-layouts: 1.99 us -> 0.68 us
  other arithmetic: 0 us -> 0.68 us
    unnamed x5 -> x1, local copies, waits for them, and re-layouts: 1.99 us -> 0.68 us
    concatenate x0 -> x1, other arithmetic: none -> 0.68 us  [body(): jnp.concatenate([partners, counts])]
where the time goes in v8:
time: 61.7 us
  Pallas kernels  60.3 us (98%)
  other arithmetic  0.68 us (1%)
  local copies, waits for them, and re-layouts  0.68 us (1%)
    pallas_call x1, Pallas kernels, body(): pl.pallas_call(functools.partial(decoder_kernel, groups, shards), out_sha...  60.3 us

profile of v8, /device:TPU:32, one launch (start us, length us, event | category | flops | bytes accessed | tf_op | source)
XLA Modules:
  0.0 61.7 jit_solution(18356820026418682079)
XLA Ops:
  0.0 0.7 %pad_add_fusion.table_ref = s32[130]{0:T(256)S(1)} fusion(s32[2]{0:T(128)} %param.12, s32[128]{0:T(128)} %param.13), kind=kLoop, calls=%fused_computation | loop fusion | flops 130 | bytes 1040 | tf_op jit(solution)/shard_map/concatenate | solution.py:607
  0.7 60.3 %decoder.1 = bf16[196,2,256]{2,1,0:T(2,128)(2,1)S(1)} custom-call(s32[130]{0:T(256)S(1)} %pad_add_fusion.table_ref, bf16[196,2,1024]{2,1,0:T(2,128)(2,1)} %bitcast.4, bf16[196,2,1024]{2,1,0:T(2,128)(2,1)} %bitcast.5, bf16[1024,256]{1,0:T(8,128)(2,1)} %query_hbm.1, bf16[1024,256]{1,0:T(8,128)(2,1)} %key_hbm.1, bf16[1024,256]{1,0:T(8,128)(2,1)} %value_hbm.1, ...), custom_call_target="tpu_custom_call" | custom-call | tf_op jit(solution)/shard_map/decoder/pallas_call | solution.py:568
  61.0 0.7 %copy.12 = bf16[2,196,256]{2,0,1:T(2,128)(2,1)} copy(bf16[2,196,256]{2,0,1:T(2,128)(2,1)S(1)} %bitcast.3) | data formatting | bytes 401408
